TPU v7x, 32 devices: a whole 2x2x4 slice. The times are simulated.
32 devices in a mesh: gy: 8 (over z, x), gx: 4 (over y, core).
Axes of the slice: x: 2, y: 2, z: 4, core: 2. Of those that a mesh axis runs over, the one named last changes fastest.
Arguments:
- imbalance: float32 [4, 1024, 2048], P(None, 'gy', 'gx'), may hold values from -9 to 9
- flow: float32 [2, 4, 1024, 2048], P(None, None, 'gy', 'gx'), may hold values from -3 to 3
- potential: float32 [4, 1024, 2048], P(None, 'gy', 'gx'), may hold values from -5 to 5
- cost: float32 [1024, 2048], P('gy', 'gx'), may hold values from 0.2 to 2
Outputs:
- flow_out: float32 [2, 4, 1024, 2048], P(None, None, 'gy', 'gx')
- potential_out: float32 [4, 1024, 2048], P(None, 'gy', 'gx')
- residual: float32 [4], replicated
All inputs are finite; a program needn't handle non-finite values.
Results may differ from a plain program's by a relative error of at most 0.0001.
Values sent between devices are 32-bit elements; how exact they have to be, the bound alone decides.
A program may use at most 64 MiB of HBM per device.

v0:
```python
import functools

import jax
import jax.numpy as jnp
from jax import lax
from jax.experimental import pallas as pl
from jax.experimental.pallas import tpu as pltpu
from jax.sharding import PartitionSpec as P

ITERS = 12
LANES = 128
GROUPS = 4
SUBS = 8

initial_step = 0.35
epsilon = 1e-06
MESH = pl.DeviceIdType.MESH


def kernel(
    ny, nx,
    imb_hbm, flow_hbm, u_hbm, cost_hbm,
    flow_hbm_out, u_hbm_out, res_out,
    imb_in, flow_in, u_in, cost_in,
    A, B, U, R, IM, CO,
    tau_ref, sig_ref,
    row_send, col_send, row_recv, col_recv, msg_send, msg_recv,
    ext_row, ext_col, ext_row_in, ext_col_in, grow, gcol,
    halo_ssem, halo_rsem, msg_ssem, msg_rsem, ext_ssem, ext_rsem, in_sem, out_sem,
):
    pairs, T, _, C = A.shape
    n = ny * nx
    G = grow.shape[0]
    gp = pairs // G
    gy, gx = lax.axis_index("gy"), lax.axis_index("gx")
    me = gy * nx + gx
    up, down, left, right = gy > 0, gy < ny - 1, gx > 0, gx < nx - 1
    f32 = jnp.float32

    K = C // LANES

    def column(ref, k):
        return ref.at[(slice(None),) * (len(ref.shape) - 1) + (pl.ds(k * LANES, LANES),)]

    fetches = [
        pltpu.make_async_copy(column(src, k), dst.at[k], in_sem.at[i, k])
        for i, (src, dst) in enumerate(((cost_hbm, cost_in), (u_hbm, u_in), (flow_hbm, flow_in), (imb_hbm, imb_in)))
        for k in range(K)
    ]
    for copy in fetches:
        copy.start()

    def gather(ref, *index):
        rows = pl.ds(index[-1], SUBS, stride=T)
        return jnp.concatenate([ref[(k,) + index[:-1] + (rows, slice(None))] for k in range(K)], axis=1)

    def scatter(ref, value, *index):
        rows = pl.ds(index[-1], SUBS, stride=T)
        for k in range(K):
            ref[(k,) + index[:-1] + (rows, slice(None))] = value[:, k * LANES:(k + 1) * LANES]

    barrier = pltpu.get_barrier_semaphore()

    def coords(offset):
        other = lax.rem(me + offset, n)
        return (other // nx, lax.rem(other, nx))

    def greet(k, c):
        pl.semaphore_signal(barrier, inc=1, device_id=coords(k), device_id_type=MESH)
        return c

    lax.fori_loop(1, n, greet, 0)

    lane = lax.broadcasted_iota(jnp.int32, (SUBS, LANES), 1)
    sub = lax.broadcasted_iota(jnp.int32, (SUBS, LANES), 0)
    subw = lax.broadcasted_iota(jnp.int32, (SUBS, C), 0)
    group, within = lane // T, lax.rem(lane, T)
    lane1, within1 = lane[0:1], within[0:1]

    def wide(x):
        return jnp.concatenate([x] * (C // LANES), axis=1)

    def row8(x, width):
        return jnp.broadcast_to(x, (SUBS, width))

    def to_left(x, entering):
        r = pltpu.roll(x, C - 1, 1)
        lanes = lax.broadcasted_iota(jnp.int32, entering.shape, 1)
        tail = jnp.where(lanes == LANES - 1, entering, r[:, C - LANES:])
        return jnp.concatenate([r[:, : C - LANES], tail], axis=1)

    def to_right(x, entering):
        r = pltpu.roll(x, 1, 1)
        head = jnp.where(lane == 0, entering, r[:, :LANES])
        return jnp.concatenate([head, r[:, LANES:]], axis=1)

    def pack_first(acc, x, t):
        v = x[:, :LANES]
        return jnp.where(lane == t, pltpu.roll(v, t, 1) if t else v, acc)

    def pack_last(acc, x, t):
        v = pltpu.roll(x[:, C - LANES:], (t + 1) % LANES, 1)
        return jnp.where(lane == t, v, acc)

    def turned(x, by):
        return x if isinstance(by, int) and by == 0 else pltpu.roll(x, by, 1)

    def place(acc, packed, p):
        return jnp.where(group == p, turned(packed, p * T), acc)

    def remote(src, dst, ssem, rsem, where):
        return pltpu.make_async_remote_copy(
            src_ref=src, dst_ref=dst, send_sem=ssem, recv_sem=rsem, device_id=where, device_id_type=MESH
        )

    def halos(slot, g):
        rows = [
            (ok_to, ok_from, remote(row_send.at[slot, k, g], row_recv.at[slot, k, g], halo_ssem.at[slot, k, g], halo_rsem.at[slot, k, g], (gy + d, gx)))
            for k, d, ok_to, ok_from in ((0, -1, up, down), (1, 1, down, up))
        ]
        cols = [
            (ok_to, ok_from, remote(col_send.at[slot, k, g], col_recv.at[slot, k, g], halo_ssem.at[slot, 2 + k, g], halo_rsem.at[slot, 2 + k, g], (gy, gx + d)))
            for k, d, ok_to, ok_from in ((0, -1, left, right), (1, 1, right, left))
        ]
        return rows + cols

    def extras():
        return [
            (down, up, remote(ext_row, ext_row_in, ext_ssem.at[0], ext_rsem.at[0], (gy + 1, gx))),
            (right, left, remote(ext_col, ext_col_in, ext_ssem.at[1], ext_rsem.at[1], (gy, gx + 1))),
        ]

    def start_all(copies):
        for ok_to, _, copy in copies:
            @pl.when(ok_to)
            def _(copy=copy):
                copy.start()

    def wait_all(copies):
        for ok_to, ok_from, copy in copies:
            @pl.when(ok_from)
            def _(copy=copy):
                copy.wait_recv()

            @pl.when(ok_to)
            def _(copy=copy):
                copy.wait_send()

    def send_message(slot, g, row):
        msg_send[slot, g] = row
        msg_recv[slot, g, me] = row

        for j in range(ny):
            y = jnp.where(gy < ny // 2, ny - 1 - j, j)
            for x in range(nx):
                @pl.when(jnp.logical_or(y != gy, gx != x))
                def _():
                    remote(
                        msg_send.at[slot, g], msg_recv.at[slot, g, me], msg_ssem.at[slot, g], msg_rsem.at[slot, g], (y, x)
                    ).start()

    def wait_message(slot, g):
        whole = msg_recv.at[slot, g, pl.ds(0, n - 1)]
        pltpu.make_async_copy(whole, whole, msg_rsem.at[slot, g]).wait()
        pltpu.make_async_copy(whole, whole, msg_ssem.at[slot, g]).wait()

    def total_rows(slot, g):
        parts = [msg_recv[slot, g, k] for k in range(n)]
        while len(parts) > 1:
            parts = [sum(parts[k + 1:k + 2], parts[k]) for k in range(0, len(parts), 2)]
        total = row8(parts[0], LANES)
        pick = jnp.where(sub < gp, sub * T + 1, (sub - gp) * T + 2)
        return row8_lanes(jnp.sum(jnp.where(lane == pick, total, 0.0), axis=1, keepdims=True))

    def each(body, init):
        return lax.fori_loop(0, gp, body, init) if gp > 1 else body(0, init)

    def row8_lanes(x):
        return jnp.broadcast_to(x, (SUBS, LANES))

    def message(first, last, sums_a, sums_b):
        return jnp.where(
            within1 == T - 1, first[SUBS - 1:SUBS],
            jnp.where(within1 == 0, last[0:1], jnp.where(within1 == 1, sums_a, sums_b)),
        )

    ones = jnp.ones((SUBS, LANES), f32)
    for copy in fetches:
        copy.wait()
    for t in range(T):
        CO[t] = gather(cost_in, t)

    def load(g, c):
        def problem(p, carry):
            packs = [ones] * 5
            q = g * gp + p
            for t in range(T):
                a, b = gather(flow_in, 0, q, t), gather(flow_in, 1, q, t)
                u = gather(u_in, q, t)
                A[q, t] = a
                B[q, t] = b
                U[q, t] = u
                IM[q, t] = gather(imb_in, q, t)
                packs[0] = pack_first(packs[0], u, t)
                for k, x in ((1, u), (2, a), (3, b), (4, CO[t])):
                    packs[k] = pack_last(packs[k], x, t)
                if t == 0:
                    row_send[0, 0, g, pl.ds(p, 1), :] = u[0:1]
                if t == T - 1:
                    row_send[0, 1, g, pl.ds(p, 1), :] = u[SUBS - 1:]
                    ext_row[0, g, pl.ds(p, 1), :] = a[SUBS - 1:]
                    ext_row[1, g, pl.ds(p, 1), :] = b[SUBS - 1:]
                    ext_row[2, g, pl.ds(p, 1), :] = CO[t][SUBS - 1:]
            return tuple(place(c, x, p) for c, x in zip(carry, packs))

        first, last, last_a, last_b, last_c = each(problem, (ones,) * 5)
        col_send[0, 0, g] = first
        col_send[0, 1, g] = last
        ext_col[0, g] = last_a
        ext_col[1, g] = last_b
        ext_col[2, g] = last_c
        return c

    lax.fori_loop(0, G, load, 0)
    tau_ref[...] = jnp.full(tau_ref.shape, initial_step, f32)
    sig_ref[...] = jnp.full(sig_ref.shape, initial_step, f32)

    for missing, refs in (
        (jnp.logical_not(down), [row_recv.at[s, 0] for s in range(2)]),
        (jnp.logical_not(up), [row_recv.at[s, 1] for s in range(2)] + [ext_row_in]),
        (jnp.logical_not(right), [col_recv.at[s, 0] for s in range(2)]),
        (jnp.logical_not(left), [col_recv.at[s, 1] for s in range(2)] + [ext_col_in]),
    ):
        @pl.when(missing)
        def _(refs=refs):
            for ref in refs:
                ref[...] = jnp.zeros(ref.shape, f32)

    pl.semaphore_wait(barrier, n - 1)
    start_all(extras())

    def corners(g):
        return [
            (ok_to, ok_from, remote(msg_send.at[0, g], msg_recv.at[0, g, me], msg_ssem.at[2 + k, g], msg_rsem.at[2 + k, g], (gy + dy, gx + dx)))
            for k, dy, dx, ok_to, ok_from in (
                (0, -1, 1, jnp.logical_and(up, right), jnp.logical_and(down, left)),
                (1, 1, -1, jnp.logical_and(down, left), jnp.logical_and(up, right)),
            )
        ]

    def announce(g, c):
        row = message(col_send[0, 0, g], col_send[0, 1, g], ones[0:1], ones[0:1])
        msg_send[0, g] = row
        start_all(halos(0, g) + corners(g))
        return c

    lax.fori_loop(0, G, announce, 0)
    wait_all(extras())
    for k in range(2):
        for g in range(G):
            grow[g, k] = ext_row_in[k, g]
            gcol[g, k] = ext_col_in[k, g]

    def above_first(a_last, g, p):
        ghost = row8(grow[g, 0, pl.ds(p, 1), :], C)
        return jnp.where(subw == 0, ghost, pltpu.roll(a_last, 1, 0))

    def shortfall(p, t, a, a_above, b, gb):
        b_left = to_right(b, pltpu.roll(gb, (LANES - t) % LANES, 1))
        return ((a - a_above) + (b - b_left)) - IM[p, t]

    def ghost_flux(g, p):
        return turned(gcol[g, 1], (LANES - p * T) % LANES)

    def begin(g, c):
        def problem(p, c):
            q = g * gp + p
            gb = ghost_flux(g, p)
            for t in range(T):
                above = A[q, t - 1] if t else above_first(A[q, T - 1], g, p)
                R[q, t] = shortfall(q, t, A[q, t], above, B[q, t], gb)
            return c

        return each(problem, c)

    lax.fori_loop(0, G, begin, 0)

    def settled(g, c):
        wait_all(halos(0, g) + corners(g))
        return c

    lax.fori_loop(0, G, settled, 0)

    results = [
        pltpu.make_async_copy(src.at[k], column(dst, k), out_sem.at[i, k])
        for i, (src, dst) in enumerate(((flow_in, flow_hbm_out), (u_in, u_hbm_out)))
        for k in range(K)
    ]

    def shrink(va, vb, t):
        f = jnp.maximum(1.0 - t * lax.rsqrt(va * va + vb * vb), 0.0)
        return f * va, f * vb

    def ghosts(slot, g):
        u = row_recv[slot, 1, g]
        sub_p, lane_p = sub[:gp], lane[:gp]
        ok = jnp.logical_and(up, right)
        corner = msg_recv[slot, g, jnp.where(ok, me - nx + 1, me)]
        corner = jnp.where(ok, corner, jnp.zeros_like(corner))
        corner = jnp.broadcast_to(corner, (gp, LANES))
        corner = jnp.sum(jnp.where(lane_p == sub_p * T + T - 1, corner, 0.0), axis=1, keepdims=True)
        u_right = to_left(u, jnp.broadcast_to(corner, (gp, LANES)))
        rate = wide(tau_ref[g, 0:gp])
        a2, b2 = shrink(
            grow[g, 0] + rate * (row_send[slot, 0, g] - u), grow[g, 1] + rate * (u_right - u), rate * ext_row_in[2, g]
        )
        grow[g, 0] = jnp.where(up, a2, jnp.zeros_like(a2))
        grow[g, 1] = jnp.where(up, b2, jnp.zeros_like(b2))
        u = col_recv[slot, 1, g]
        ok = jnp.logical_and(down, left)
        corner = msg_recv[slot, g, jnp.where(ok, me + nx - 1, me)]
        corner = jnp.where(ok, corner, jnp.zeros_like(corner))
        turn = jnp.where(sub == SUBS - 1, row8(corner, LANES), pltpu.roll(u, SUBS - 1, 0))
        u_down = jnp.where(within == T - 1, pltpu.roll(turn, T - 1, 1), pltpu.roll(u, LANES - 1, 1))
        rate = row8(tau_ref[g, 0:1], LANES)
        for p in range(1, gp):
            rate = jnp.where(group == p, row8(tau_ref[g, p:p + 1], LANES), rate)
        a2, b2 = shrink(
            gcol[g, 0] + rate * (u_down - u), gcol[g, 1] + rate * (col_send[slot, 0, g] - u), rate * ext_col_in[2, g]
        )
        gcol[g, 0] = jnp.where(left, a2, jnp.zeros_like(a2))
        gcol[g, 1] = jnp.where(left, b2, jnp.zeros_like(b2))

    def adapt(slot, g):
        wait_all(halos(slot, g))
        wait_message(slot, g)
        sums = total_rows(slot, g)
        primal, dual_sums = sums, pltpu.roll(sums, SUBS - gp, 0)
        s = jnp.sqrt(jnp.sqrt((primal + epsilon) / (dual_sums + epsilon)))
        tau_ref[g] = tau_ref[g] / s
        sig_ref[g] = sig_ref[g] * s

    def sweep(g, slot, closing):
        other = 1 - slot
        ghosts(slot, g)

        def problem(p, carry):
            sums_a, sums_b, first, last = carry
            q = g * gp + p
            tau = wide(row8(tau_ref[g, pl.ds(p, 1), :], LANES))
            sigma = wide(row8(sig_ref[g, pl.ds(p, 1), :], LANES))
            gb = ghost_flux(g, p)
            hc = pltpu.roll(col_recv[slot, 0, g], LANES - 1 - p * T, 1)
            acc_p = jnp.zeros((SUBS, C), f32)
            acc_d = jnp.zeros((SUBS, C), f32)
            pack_f, pack_l = ones, ones

            def dual(t, a2, above, b2, u):
                nonlocal acc_p, acc_d, pack_f, pack_l
                r2 = shortfall(q, t, a2, above, b2, gb)
                change = sigma * (r2 + (r2 - R[q, t]))
                u2 = u + change
                if closing:
                    acc_d = acc_d + r2 * r2
                    scatter(u_in, u2, q, t)
                    return
                acc_d = acc_d + change * change
                R[q, t] = r2
                U[q, t] = u2
                pack_f = pack_first(pack_f, u2, t)
                pack_l = pack_last(pack_l, u2, t)
                if t == 0:
                    row_send[other, 0, g, pl.ds(p, 1), :] = u2[0:1]
                if t == T - 1:
                    row_send[other, 1, g, pl.ds(p, 1), :] = u2[SUBS - 1:]

            u_first = u = U[q, 0]
            for t in range(T):
                if t < T - 1:
                    u_down = U[q, t + 1]
                else:
                    below = row8(row_recv[slot, 0, g, pl.ds(p, 1), :], C)
                    u_down = jnp.where(subw == SUBS - 1, below, pltpu.roll(u_first, SUBS - 1, 0))
                u_right = to_left(u, pltpu.roll(hc, (LANES - t) % LANES, 1))
                a, b = A[q, t], B[q, t]
                a2, b2 = shrink(a + tau * (u_down - u), b + tau * (u_right - u), tau * CO[t])
                if closing:
                    scatter(flow_in, a2, 0, q, t)
                    scatter(flow_in, b2, 1, q, t)
                else:
                    A[q, t] = a2
                    B[q, t] = b2
                    da, db = a2 - a, b2 - b
                    acc_p = acc_p + (da * da + db * db)
                if t:
                    dual(t, a2, above, b2, u)
                else:
                    a_first, b_first = a2, b2
                above, u = a2, u_down
            dual(0, a_first, above_first(above, g, p), b_first, u_first)

            def settle(sums, acc):
                part = jnp.sum(jnp.sum(acc, axis=0, keepdims=True), axis=1, keepdims=True)
                return jnp.where(group[0:1] == p, jnp.broadcast_to(part, (1, LANES)), sums)

            sums_b = settle(sums_b, acc_d)
            if closing:
                return sums_a, sums_b, first, last
            return settle(sums_a, acc_p), sums_b, place(first, pack_f, p), place(last, pack_l, p)

        start = (ones[0:1], ones[0:1], ones, ones)
        sums_a, sums_b, first, last = each(problem, start)
        if not closing:
            col_send[other, 0, g] = first
            col_send[other, 1, g] = last
        send_message(other, g, message(first, last, sums_a, sums_b))
        if not closing:
            start_all(halos(other, g))

    def turn(i, c):
        slot = lax.rem(i, 2)

        def one(g, c):
            @pl.when(i > 0)
            def _():
                adapt(slot, g)

            sweep(g, slot, False)
            return c

        return lax.fori_loop(0, G, one, c)

    lax.fori_loop(0, ITERS - 1, turn, 0)
    slot = (ITERS - 1) % 2

    def close(g, c):
        adapt(slot, g)
        sweep(g, slot, True)
        return c

    lax.fori_loop(0, G, close, 0)
    for copy in results:
        copy.start()
    cells = T * SUBS * C * n
    for g in range(G):
        wait_message(1 - slot, g)
        res_out[g] = total_rows(1 - slot, g) / cells
    for copy in results:
        copy.wait()


def local(ny, nx, imbalance, flow, potential, cost):
    pairs, rows, cols = imbalance.shape
    T = rows // SUBS
    n = ny * nx
    assert 2 * pairs <= SUBS and pairs * T <= LANES and T >= 4
    G = GROUPS if pairs % GROUPS == 0 else 1
    gp = pairs // G
    f32 = jnp.float32
    block = (pairs, T, SUBS, cols)
    packed = (SUBS, LANES)
    K = cols // LANES
    hbm = pl.BlockSpec(memory_space=pltpu.HBM)
    flow_out, u_out, res = pl.pallas_call(
        functools.partial(kernel, ny, nx),
        out_shape=(
            jax.ShapeDtypeStruct(flow.shape, f32),
            jax.ShapeDtypeStruct(potential.shape, f32),
            jax.ShapeDtypeStruct((G,) + packed, f32),
        ),
        in_specs=[hbm] * 4,
        out_specs=(hbm, hbm, pl.BlockSpec(memory_space=pltpu.VMEM)),
        scratch_shapes=[
            pltpu.VMEM((K, pairs, rows, LANES), f32), pltpu.VMEM((K, 2, pairs, rows, LANES), f32),
            pltpu.VMEM((K, pairs, rows, LANES), f32), pltpu.VMEM((K, rows, LANES), f32),
            pltpu.VMEM(block, f32), pltpu.VMEM(block, f32), pltpu.VMEM(block, f32), pltpu.VMEM(block, f32),
            pltpu.VMEM(block, f32), pltpu.VMEM(block[1:], f32),
            pltpu.VMEM((G,) + packed, f32), pltpu.VMEM((G,) + packed, f32),
            pltpu.VMEM((2, 2, G, gp, cols), f32), pltpu.VMEM((2, 2, G) + packed, f32),
            pltpu.VMEM((2, 2, G, gp, cols), f32), pltpu.VMEM((2, 2, G) + packed, f32),
            pltpu.VMEM((2, G, 1, LANES), f32), pltpu.VMEM((2, G, n, 1, LANES), f32),
            pltpu.VMEM((3, G, gp, cols), f32), pltpu.VMEM((3, G) + packed, f32),
            pltpu.VMEM((3, G, gp, cols), f32), pltpu.VMEM((3, G) + packed, f32),
            pltpu.VMEM((G, 2, gp, cols), f32), pltpu.VMEM((G, 2) + packed, f32),
            pltpu.SemaphoreType.DMA((2, 4, G)), pltpu.SemaphoreType.DMA((2, 4, G)),
            pltpu.SemaphoreType.DMA((4, G)), pltpu.SemaphoreType.DMA((4, G)),
            pltpu.SemaphoreType.DMA((2,)), pltpu.SemaphoreType.DMA((2,)),
            pltpu.SemaphoreType.DMA((4, K)), pltpu.SemaphoreType.DMA((2, K)),
        ],
        compiler_params=pltpu.CompilerParams(
            collective_id=0, has_side_effects=True, vmem_limit_bytes=48 * 1024 * 1024
        ),
    )(*(pltpu.with_memory_space_constraint(x, pltpu.HBM) for x in (imbalance, flow, potential, cost)))
    return flow_out, u_out, res[:, gp:2 * gp, 0].reshape(pairs)


def solution(mesh):
    placed = (P(None, "gy", "gx"), P(None, None, "gy", "gx"), P(None, "gy", "gx"), P("gy", "gx"))
    return jax.shard_map(
        functools.partial(local, mesh.shape["gy"], mesh.shape["gx"]),
        mesh=mesh,
        in_specs=placed,
        out_specs=(P(None, None, "gy", "gx"), P(None, "gy", "gx"), P()),
        check_vma=False,
    )
```

profile of v0, /device:TPU:0, one launch (start us, length us, event | category | flops | bytes accessed | tf_op | source)
XLA Modules:
  0.0 77.7 jit_solution(5154616623095843889)
XLA Ops:
  0.6 74.2 %shard_map.67 = (f32[2,4,128,512]{3,2,1,0:T(8,128)S(1)}, f32[4,128,512]{2,1,0:T(8,128)S(1)}, f32[4,8,128]{2,1,0:T(8,128)S(1)}) custom-call(f32[4,128,512]{2,1,0:T(8,128)} %imb_hbm.1, f32[2,4,128,512]{3,2,1,0:T(8,128)} %flow_hbm.1, f32[4,128,512]{2,1,0:T(8,128)} %u_hbm.1, f32[128,512]{1,0:T(8,128)} %cost_hbm.1), custom_call_target="tpu_custom_call" | custom-call | tf_op jit(solution)/shard_map/pallas_call | solution.py:464
  74.8 0.6 slice_reduce_fusion
  75.5 1.3 %copy.9 = f32[2,4,128,512]{3,2,1,0:T(8,128)} copy(f32[2,4,128,512]{3,2,1,0:T(8,128)S(1)} %get-tuple-element.12) | data formatting | bytes 4194304
  76.8 1.0 %copy.10 = f32[4,128,512]{2,1,0:T(8,128)} copy(f32[4,128,512]{2,1,0:T(8,128)S(1)} %get-tuple-element.13) | data formatting | bytes 2097152
where the time goes:
time: 77.9 us; the launch traced here: 77.7 us
  Pallas kernels  74.2 us (95%)
  local copies, waits for them, and re-layouts  2.91 us (4%)
    pallas_call x1, Pallas kernels, local(): pl.pallas_call(functools.partial(kernel, ny, nx), out_shape=(jax.ShapeDty...  74.2 us
    unnamed x2, local copies, waits for them, and re-layouts  2.29 us

commit v1 on v0

v1 whole, which is shorter than its diff:
```python
import functools

import jax
import jax.numpy as jnp
from jax import lax
from jax.experimental import pallas as pl
from jax.experimental.pallas import tpu as pltpu
from jax.sharding import PartitionSpec as P

ITERS = 12
LANES = 128
SUBS = 8

initial_step = 0.35
epsilon = 1e-06
MESH = pl.DeviceIdType.MESH


def kernel(
    ny, nx,
    imb_hbm, flow_hbm, u_hbm, cost_hbm,
    flow_hbm_out, u_hbm_out, res_out,
    imb_in, flow_in, u_in, cost_in,
    A, B, U, E, Q, CH, GA, GB, IM, CO,
    tau_ref, sig_ref,
    row_send, col_send, row_recv, col_recv, corner_recv, msg_send, msg_recv,
    ext_row, ext_col, ext_row_in, ext_col_in, cost_row, cost_col, cost_row_in, cost_col_in,
    grow, gcol, slope_row, slope_col,
    halo_ssem, halo_rsem, msg_ssem, msg_rsem, ext_ssem, ext_rsem, in_sem, out_sem,
):
    G, T, _, C = A.shape
    n = ny * nx
    rows = T * SUBS
    gy, gx = lax.axis_index("gy"), lax.axis_index("gx")
    me = gy * nx + gx
    up, down, left, right = gy > 0, gy < ny - 1, gx > 0, gx < nx - 1
    f32 = jnp.float32
    K = C // LANES

    def piece(ref, k):
        return ref.at[(slice(None),) * (len(ref.shape) - 1) + (pl.ds(k * LANES, LANES),)]

    def fetch(i, g, k):
        if i == 0:
            return pltpu.make_async_copy(piece(cost_hbm, k), cost_in.at[k], in_sem.at[0, 0, k])
        if i == 1:
            return pltpu.make_async_copy(piece(u_hbm.at[g], k), u_in.at[k, g], in_sem.at[1, g, k])
        if i == 2:
            return pltpu.make_async_copy(
                flow_hbm.at[:, g, :, pl.ds(k * LANES, LANES)], flow_in.at[k, :, g], in_sem.at[2, g, k]
            )
        return pltpu.make_async_copy(piece(imb_hbm.at[g], k), imb_in.at[k, g], in_sem.at[3, g, k])

    def start_fetch(i, g):
        for k in range(K):
            fetch(i, g, k).start()

    def wait_fetch(i, g):
        for k in range(K):
            fetch(i, g, k).wait()

    half = ny // 2
    low = gy < half
    xs = [lax.rem(gx + d, nx) for d in range(nx)]
    order = sorted(range(nx), key=lambda d: -min(d, nx - d))
    places = [(jnp.where(low, ny - 1 - j, j), xs[d]) for j in range(half) for d in order]
    high = jnp.where(low, ny - 1 - gy, gy) - half
    for k in range(1, ny - half):
        y = half + lax.rem(high + k, ny - half)
        places += [(jnp.where(low, ny - 1 - y, y), xs[d]) for d in order]
    places += [(gy, xs[d]) for d in order if d]

    barrier = pltpu.get_barrier_semaphore()
    for where in places:
        pl.semaphore_signal(barrier, inc=1, device_id=where, device_id_type=MESH)

    start_fetch(0, 0)
    start_fetch(1, 0)
    start_fetch(2, 0)

    def later(g, c):
        start_fetch(1, g)
        start_fetch(2, g)
        return c

    lax.fori_loop(1, G, later, 0)

    def last(g, c):
        start_fetch(3, g)
        return c

    lax.fori_loop(0, G, last, 0)

    def gather(ref, *index):
        at = pl.ds(index[-1], SUBS, stride=T)
        return jnp.concatenate([ref[(k,) + index[:-1] + (at, slice(None))] for k in range(K)], axis=1)

    def scatter(ref, value, *index):
        at = pl.ds(index[-1], SUBS, stride=T)
        for k in range(K):
            ref[(k,) + index[:-1] + (at, slice(None))] = value[:, k * LANES:(k + 1) * LANES]

    def line(ref, *index):
        return jnp.concatenate([ref[(k,) + index[:-1] + (pl.ds(index[-1], 1), slice(None))] for k in range(K)], axis=1)

    lane = lax.broadcasted_iota(jnp.int32, (SUBS, LANES), 1)
    sub = lax.broadcasted_iota(jnp.int32, (SUBS, LANES), 0)
    subw = lax.broadcasted_iota(jnp.int32, (SUBS, C), 0)
    ones = jnp.ones((SUBS, LANES), f32)

    def wide(x):
        return jnp.concatenate([x] * K, axis=1)

    def row8(x):
        return jnp.broadcast_to(x, (SUBS, x.shape[1]))

    def turn_lanes(x, by):
        return pltpu.roll(x, by % LANES, 1) if by % LANES else x

    def to_left(x, entering):
        r = pltpu.roll(x, C - 1, 1)
        lanes = lax.broadcasted_iota(jnp.int32, entering.shape, 1)
        tail = jnp.where(lanes == LANES - 1, entering, r[:, C - LANES:])
        return jnp.concatenate([r[:, : C - LANES], tail], axis=1)

    def to_right(x, entering):
        r = pltpu.roll(x, 1, 1)
        head = jnp.where(lane == 0, entering, r[:, :LANES])
        return jnp.concatenate([head, r[:, LANES:]], axis=1)

    def pack_first(acc, v, t):
        return jnp.where(lane == t, turn_lanes(v, t), acc)

    def pack_last(acc, v, t):
        return jnp.where(lane == t, turn_lanes(v, t + 1), acc)

    def remote(src, dst, ssem, rsem, where):
        return pltpu.make_async_remote_copy(
            src_ref=src, dst_ref=dst, send_sem=ssem, recv_sem=rsem, device_id=where, device_id_type=MESH
        )

    def halos(slot, g):
        sems = lambda k: (halo_ssem.at[slot, k, g], halo_rsem.at[slot, k, g])
        head, tail = row_send.at[slot, 0, g], row_send.at[slot, 1, g]
        return [
            (up, down, remote(head, row_recv.at[slot, 0, g], *sems(0), (gy - 1, gx))),
            (down, up, remote(tail, row_recv.at[slot, 1, g], *sems(1), (gy + 1, gx))),
            (left, right, remote(col_send.at[slot, 0, g], col_recv.at[slot, 0, g], *sems(2), (gy, gx - 1))),
            (right, left, remote(col_send.at[slot, 1, g], col_recv.at[slot, 1, g], *sems(3), (gy, gx + 1))),
            (
                jnp.logical_and(down, left), jnp.logical_and(up, right),
                remote(tail.at[:, pl.ds(0, LANES)], corner_recv.at[slot, 0, g], *sems(4), (gy + 1, gx - 1)),
            ),
            (
                jnp.logical_and(up, right), jnp.logical_and(down, left),
                remote(head.at[:, pl.ds(C - LANES, LANES)], corner_recv.at[slot, 1, g], *sems(5), (gy - 1, gx + 1)),
            ),
        ]

    def extras(g):
        return [
            (down, up, remote(ext_row.at[g], ext_row_in.at[g], ext_ssem.at[0, g], ext_rsem.at[0, g], (gy + 1, gx))),
            (right, left, remote(ext_col.at[g], ext_col_in.at[g], ext_ssem.at[1, g], ext_rsem.at[1, g], (gy, gx + 1))),
        ]

    def prices():
        return [
            (down, up, remote(cost_row, cost_row_in, ext_ssem.at[0, G], ext_rsem.at[0, G], (gy + 1, gx))),
            (right, left, remote(cost_col, cost_col_in, ext_ssem.at[1, G], ext_rsem.at[1, G], (gy, gx + 1))),
        ]

    def start_all(copies):
        for ok_to, _, copy in copies:
            @pl.when(ok_to)
            def _(copy=copy):
                copy.start()

    def wait_all(copies):
        for ok_to, ok_from, copy in copies:
            @pl.when(ok_from)
            def _(copy=copy):
                copy.wait_recv()

            @pl.when(ok_to)
            def _(copy=copy):
                copy.wait_send()

    def send_message(slot, g, row):
        msg_send[slot, g] = row
        msg_recv[slot, g, me] = row
        for where in places:
            remote(
                msg_send.at[slot, g], msg_recv.at[slot, g, me], msg_ssem.at[slot, g], msg_rsem.at[slot, g], where
            ).start()

    def wait_message(slot, g):
        whole = msg_recv.at[slot, g, pl.ds(0, n - 1)]
        pltpu.make_async_copy(whole, whole, msg_rsem.at[slot, g]).wait()
        pltpu.make_async_copy(whole, whole, msg_ssem.at[slot, g]).wait()

    def totals(slot, g):
        parts = [msg_recv[slot, g, k] for k in range(n)]
        while len(parts) > 1:
            parts = [sum(parts[k + 1:k + 2], parts[k]) for k in range(0, len(parts), 2)]
        both = row8(parts[0])
        first = lane < LANES // 2
        return [
            jnp.sum(jnp.where(keep, both, 0.0), axis=1, keepdims=True) for keep in (first, jnp.logical_not(first))
        ]

    def fold(x, y):
        x, y = (sum((v[:, k * LANES:(k + 1) * LANES] for k in range(1, K)), v[:, :LANES]) for v in (x, y))
        first = lane < LANES // 2
        z = jnp.where(first, x, y) + pltpu.roll(jnp.where(first, y, x), LANES // 2, 1)
        for step in (4, 2, 1):
            z = z + pltpu.roll(z, step, 0)
        return z[0:1]


    def edges(g, c):
        wait_fetch(1, g)
        packs = [ones] * 4
        row_send[0, 0, g] = line(u_in, g, 0)
        row_send[0, 1, g] = line(u_in, g, rows - 1)
        for t in range(T):
            at = pl.ds(t, SUBS, stride=T)
            packs[0] = pack_first(packs[0], u_in[0, g, at, :], t)
            packs[1] = pack_last(packs[1], u_in[K - 1, g, at, :], t)
        wait_fetch(2, g)
        for t in range(T):
            at = pl.ds(t, SUBS, stride=T)
            packs[2] = pack_last(packs[2], flow_in[K - 1, 0, g, at, :], t)
            packs[3] = pack_last(packs[3], flow_in[K - 1, 1, g, at, :], t)
        col_send[0, 0, g] = packs[0]
        col_send[0, 1, g] = packs[1]
        for k in range(2):
            ext_col[g, k] = packs[2 + k]
            ext_row[g, k] = line(flow_in, k, g, rows - 1)
        return c

    wait_fetch(0, 0)
    pack = ones
    for t in range(T):
        CO[t] = gather(cost_in, t)
        pack = pack_last(pack, CO[t][:, C - LANES:], t)
    cost_col[...] = pack
    cost_row[...] = line(cost_in, rows - 1)
    lax.fori_loop(0, G, edges, 0)

    for missing, refs in (
        (jnp.logical_not(down), [row_recv.at[s, 0] for s in range(2)]),
        (jnp.logical_not(up), [row_recv.at[s, 1] for s in range(2)] + [ext_row_in]),
        (jnp.logical_not(right), [col_recv.at[s, 0] for s in range(2)]),
        (jnp.logical_not(left), [col_recv.at[s, 1] for s in range(2)] + [ext_col_in]),
        (jnp.logical_not(jnp.logical_and(up, right)), [corner_recv.at[s, 0] for s in range(2)]),
        (jnp.logical_not(jnp.logical_and(down, left)), [corner_recv.at[s, 1] for s in range(2)]),
    ):
        @pl.when(missing)
        def _(refs=refs):
            for ref in refs:
                ref[...] = jnp.zeros(ref.shape, f32)

    for missing, ref in ((jnp.logical_not(up), cost_row_in), (jnp.logical_not(left), cost_col_in)):
        @pl.when(missing)
        def _(ref=ref):
            ref[...] = jnp.ones(ref.shape, f32)

    pl.semaphore_wait(barrier, n - 1)
    start_all(prices())

    def announce(g, c):
        start_all(halos(0, g) + extras(g))
        return c

    lax.fori_loop(0, G, announce, 0)

    def load(g, c):
        wait_fetch(3, g)
        for t in range(T):
            A[g, t] = gather(flow_in, 0, g, t)
            B[g, t] = gather(flow_in, 1, g, t)
            U[g, t] = gather(u_in, g, t)
            IM[g, t] = gather(imb_in, g, t)
        return c

    lax.fori_loop(0, G, load, 0)

    def above_first(a_last, ghost):
        return jnp.where(subw == 0, row8(ghost), pltpu.roll(a_last, 1, 0))

    def divergence(t, a, above, b, gb):
        return ((a - above) + (b - to_right(b, turn_lanes(gb, -t))))

    def begin(g):
        wait_all(extras(g))
        for k in range(2):
            grow[g, k] = ext_row_in[g, k]
            gcol[g, k] = ext_col_in[g, k]
        gb = gcol[g, 1]
        for t in range(T):
            above = A[g, t - 1] if t else above_first(A[g, T - 1], grow[g, 0])
            E[g, t] = divergence(t, A[g, t], above, B[g, t], gb) + IM[g, t]

    def slopes(slot, g):
        wait_all(halos(slot, g))
        u = row_recv[slot, 1, g]
        u_right = to_left(u, turn_lanes(corner_recv[slot, 0, g], LANES - 1))
        zero = jnp.zeros_like(u)
        slope_row[g, 0] = jnp.where(up, row_send[slot, 0, g] - u, zero)
        slope_row[g, 1] = jnp.where(up, u_right - u, zero)
        u = col_recv[slot, 1, g]
        turn = turn_lanes(pltpu.roll(u, SUBS - 1, 0), T - 1)
        turn = jnp.where(sub == SUBS - 1, row8(turn_lanes(corner_recv[slot, 1, g], T)), turn)
        u_down = jnp.where(lane == T - 1, turn, turn_lanes(u, -1))
        zero = jnp.zeros_like(u)
        slope_col[g, 0] = jnp.where(left, u_down - u, zero)
        slope_col[g, 1] = jnp.where(left, col_send[slot, 0, g] - u, zero)
        below = row8(row_recv[slot, 0, g])
        beside = col_recv[slot, 0, g]
        first = u = U[g, 0]
        for t in range(T):
            if t < T - 1:
                u_down = U[g, t + 1]
            else:
                u_down = jnp.where(subw == SUBS - 1, below, pltpu.roll(first, SUBS - 1, 0))
            GA[g, t] = u_down - u
            GB[g, t] = to_left(u, turn_lanes(beside, LANES - 1 - t)) - u
            u = u_down

    def shrink(va, vb, t):
        f = jnp.maximum(1.0 - t * lax.rsqrt(va * va + vb * vb), 0.0)
        return f * va, f * vb

    def adapt(slot, g):
        wait_message(slot, g)
        primal, dual = (jnp.broadcast_to(v, (SUBS, LANES)) + epsilon for v in totals(slot, g))
        root = lax.rsqrt(primal) * (dual * lax.rsqrt(dual))
        s = lax.rsqrt(root)
        tau = tau_ref[g] * (root * s)
        sigma = sig_ref[g] * s
        tau_ref[g] = tau
        sig_ref[g] = sigma
        return tau, sigma

    def sweep(g, other, tau, sigma, closing):
        wtau, wsigma = wide(tau), wide(sigma)
        tau1 = wtau[0:1]
        ghost_a, ghost_b = shrink(
            grow[g, 0] + tau1 * slope_row[g, 0], grow[g, 1] + tau1 * slope_row[g, 1], tau1 * cost_row_in[...]
        )
        side_a, side_b = shrink(
            gcol[g, 0] + tau * slope_col[g, 0], gcol[g, 1] + tau * slope_col[g, 1], tau * cost_col_in[...]
        )
        grow[g, 0] = ghost_a
        grow[g, 1] = ghost_b
        gcol[g, 0] = side_a
        gcol[g, 1] = side_b
        acc_p = jnp.zeros((SUBS, C), f32)
        acc_d = jnp.zeros((SUBS, C), f32)

        def dual(t, a2, above, b2):
            nonlocal acc_d
            q2 = divergence(t, a2, above, b2, side_b)
            change = wsigma * ((q2 + q2) - E[g, t])
            CH[g, t] = change
            if closing:
                miss = q2 - IM[g, t]
                acc_d = acc_d + miss * miss
            else:
                Q[g, t] = q2
                acc_d = acc_d + change * change

        for t in range(T):
            a, b = A[g, t], B[g, t]
            a2, b2 = shrink(a + wtau * GA[g, t], b + wtau * GB[g, t], wtau * CO[t])
            if closing:
                scatter(flow_in, a2, 0, g, t)
                scatter(flow_in, b2, 1, g, t)
            else:
                A[g, t] = a2
                B[g, t] = b2
                da, db = a2 - a, b2 - b
                acc_p = acc_p + (da * da + db * db)
            if t:
                dual(t, a2, above, b2)
            else:
                a_first, b_first = a2, b2
            above = a2
        dual(0, a_first, above_first(above, ghost_a), b_first)
        send_message(other, g, fold(acc_p, acc_d))

    def settle(other, g):
        pack_f, pack_l = ones, ones
        for t in range(T):
            u2 = U[g, t] + CH[g, t]
            U[g, t] = u2
            E[g, t] = Q[g, t] + IM[g, t]
            pack_f = pack_first(pack_f, u2[:, :LANES], t)
            pack_l = pack_last(pack_l, u2[:, C - LANES:], t)
            if t == 0:
                row_send[other, 0, g] = u2[0:1]
            if t == T - 1:
                row_send[other, 1, g] = u2[SUBS - 1:]
        col_send[other, 0, g] = pack_f
        col_send[other, 1, g] = pack_l
        start_all(halos(other, g))

    wait_all(prices())

    def opening(g, c):
        begin(g)
        slopes(0, g)
        step = jnp.full((SUBS, LANES), initial_step, f32)
        tau_ref[g] = step
        sig_ref[g] = step
        sweep(g, 1, step, step, False)
        settle(1, g)
        return c

    lax.fori_loop(0, G, opening, 0)
    slopes(1, 0)

    def turn(i, c):
        slot = lax.rem(i, 2)
        other = 1 - slot

        def one(g, c):
            tau, sigma = adapt(slot, g)
            sweep(g, other, tau, sigma, False)
            settle(other, g)
            slopes(jnp.where(g == G - 1, other, slot), lax.rem(g + 1, G))
            return c

        return lax.fori_loop(0, G, one, c)

    lax.fori_loop(1, ITERS - 1, turn, 0)
    slot = (ITERS - 1) % 2

    def close(g, c):
        tau, sigma = adapt(slot, g)
        sweep(g, 1 - slot, tau, sigma, True)

        @pl.when(g < G - 1)
        def _():
            slopes(slot, g + 1)

        for t in range(T):
            scatter(u_in, U[g, t] + CH[g, t], g, t)
        return c

    lax.fori_loop(0, G, close, 0)
    results = [
        pltpu.make_async_copy(src.at[k], piece(dst, k), out_sem.at[i, k])
        for i, (src, dst) in enumerate(((flow_in, flow_hbm_out), (u_in, u_hbm_out)))
        for k in range(K)
    ]
    for copy in results:
        copy.start()
    cells = T * SUBS * C * n
    for g in range(G):
        wait_message(1 - slot, g)
        res_out[g] = jnp.broadcast_to(totals(1 - slot, g)[1], (SUBS, LANES)) / cells
    for copy in results:
        copy.wait()


def local(ny, nx, imbalance, flow, potential, cost):
    pairs, rows, cols = imbalance.shape
    T = rows // SUBS
    n = ny * nx
    assert rows % SUBS == 0 and cols % LANES == 0 and 4 <= T <= LANES and ny % 2 == 0
    G = pairs
    f32 = jnp.float32
    block = (pairs, T, SUBS, cols)
    packed = (SUBS, LANES)
    K = cols // LANES
    hbm = pl.BlockSpec(memory_space=pltpu.HBM)
    flow_out, u_out, res = pl.pallas_call(
        functools.partial(kernel, ny, nx),
        out_shape=(
            jax.ShapeDtypeStruct(flow.shape, f32),
            jax.ShapeDtypeStruct(potential.shape, f32),
            jax.ShapeDtypeStruct((G,) + packed, f32),
        ),
        in_specs=[hbm] * 4,
        out_specs=(hbm, hbm, pl.BlockSpec(memory_space=pltpu.VMEM)),
        scratch_shapes=[
            pltpu.VMEM((K, pairs, rows, LANES), f32), pltpu.VMEM((K, 2, pairs, rows, LANES), f32),
            pltpu.VMEM((K, pairs, rows, LANES), f32), pltpu.VMEM((K, rows, LANES), f32),
        ] + [pltpu.VMEM(block, f32)] * 9 + [
            pltpu.VMEM(block[1:], f32),
            pltpu.VMEM((G,) + packed, f32), pltpu.VMEM((G,) + packed, f32),
            pltpu.VMEM((2, 2, G, 1, cols), f32), pltpu.VMEM((2, 2, G) + packed, f32),
            pltpu.VMEM((2, 2, G, 1, cols), f32), pltpu.VMEM((2, 2, G) + packed, f32),
            pltpu.VMEM((2, 2, G, 1, LANES), f32),
            pltpu.VMEM((2, G, 1, LANES), f32), pltpu.VMEM((2, G, n, 1, LANES), f32),
            pltpu.VMEM((G, 2, 1, cols), f32), pltpu.VMEM((G, 2) + packed, f32),
            pltpu.VMEM((G, 2, 1, cols), f32), pltpu.VMEM((G, 2) + packed, f32),
            pltpu.VMEM((1, cols), f32), pltpu.VMEM(packed, f32),
            pltpu.VMEM((1, cols), f32), pltpu.VMEM(packed, f32),
            pltpu.VMEM((G, 2, 1, cols), f32), pltpu.VMEM((G, 2) + packed, f32),
            pltpu.VMEM((G, 2, 1, cols), f32), pltpu.VMEM((G, 2) + packed, f32),
            pltpu.SemaphoreType.DMA((2, 6, G)), pltpu.SemaphoreType.DMA((2, 6, G)),
            pltpu.SemaphoreType.DMA((2, G)), pltpu.SemaphoreType.DMA((2, G)),
            pltpu.SemaphoreType.DMA((2, G + 1)), pltpu.SemaphoreType.DMA((2, G + 1)),
            pltpu.SemaphoreType.DMA((4, G, K)), pltpu.SemaphoreType.DMA((2, K)),
        ],
        compiler_params=pltpu.CompilerParams(
            collective_id=0, has_side_effects=True, vmem_limit_bytes=48 * 1024 * 1024
        ),
    )(*(pltpu.with_memory_space_constraint(x, pltpu.HBM) for x in (imbalance, flow, potential, cost)))
    return flow_out, u_out, res[:, 0, 0]


def solution(mesh):
    placed = (P(None, "gy", "gx"), P(None, None, "gy", "gx"), P(None, "gy", "gx"), P("gy", "gx"))
    return jax.shard_map(
        functools.partial(local, mesh.shape["gy"], mesh.shape["gx"]),
        mesh=mesh,
        in_specs=placed,
        out_specs=(P(None, None, "gy", "gx"), P(None, "gy", "gx"), P()),
        check_vma=False,
    )
```

time: 77.9 us -> 76.2 us (0.978)
  Pallas kernels: 74.2 us -> 72.5 us
    pallas_call x1, Pallas kernels: 74.2 us -> 72.5 us  [local(): pl.pallas_call(functools.partial(kernel, ny, nx), out_shape=(jax.ShapeDty...]
where the time goes in v1:
time: 76.2 us; the launch traced here: 76 us
  Pallas kernels  72.5 us (95%)
  local copies, waits for them, and re-layouts  2.91 us (4%)
    pallas_call x1, Pallas kernels, local(): pl.pallas_call(functools.partial(kernel, ny, nx), out_shape=(jax.ShapeDty...  72.5 us
    unnamed x2, local copies, waits for them, and re-layouts  2.29 us

profile of v1, /device:TPU:0, one launch (start us, length us, event | category | flops | bytes accessed | tf_op | source)
XLA Modules:
  0.0 76.0 jit_solution(4184970277389877715)
XLA Ops:
  0.6 72.5 %shard_map.67 = (f32[2,4,128,512]{3,2,1,0:T(8,128)S(1)}, f32[4,128,512]{2,1,0:T(8,128)S(1)}, f32[4,8,128]{2,1,0:T(8,128)S(1)}) custom-call(f32[4,128,512]{2,1,0:T(8,128)} %imb_hbm.1, f32[2,4,128,512]{3,2,1,0:T(8,128)} %flow_hbm.1, f32[4,128,512]{2,1,0:T(8,128)} %u_hbm.1, f32[128,512]{1,0:T(8,128)} %cost_hbm.1), custom_call_target="tpu_custom_call" | custom-call | tf_op jit(solution)/shard_map/pallas_call | solution.py:478
  73.1 0.6 slice_reduce_fusion
  73.7 1.3 %copy.9 = f32[2,4,128,512]{3,2,1,0:T(8,128)} copy(f32[2,4,128,512]{3,2,1,0:T(8,128)S(1)} %get-tuple-element.12) | data formatting | bytes 4194304
  75.0 1.0 %copy.10 = f32[4,128,512]{2,1,0:T(8,128)} copy(f32[4,128,512]{2,1,0:T(8,128)S(1)} %get-tuple-element.13) | data formatting | bytes 2097152

commit v2 on v1

--- a/solution.py
+++ b/solution.py
@@ -21,12 +21,13 @@
     imb_hbm, flow_hbm, u_hbm, cost_hbm,
     flow_hbm_out, u_hbm_out, res_out,
     imb_in, flow_in, u_in, cost_in,
-    A, B, U, E, Q, CH, GA, GB, IM, CO,
+    A, B, U, E, W, GA, GB, IM, CO,
     tau_ref, sig_ref,
     row_send, col_send, row_recv, col_recv, corner_recv, msg_send, msg_recv,
     ext_row, ext_col, ext_row_in, ext_col_in, cost_row, cost_col, cost_row_in, cost_col_in,
     grow, gcol, slope_row, slope_col,
-    halo_ssem, halo_rsem, msg_ssem, msg_rsem, ext_ssem, ext_rsem, in_sem, out_sem,
+    res_row,
+    halo_ssem, halo_rsem, msg_ssem, msg_rsem, ext_ssem, ext_rsem, in_sem, out_sem, plane_sem,
 ):
     G, T, _, C = A.shape
     n = ny * nx
@@ -70,13 +71,33 @@
         places += [(jnp.where(low, ny - 1 - y, y), xs[d]) for d in order]
     places += [(gy, xs[d]) for d in order if d]
 
+    start_fetch(1, 0)
+    start_fetch(0, 0)
+    start_fetch(2, 0)
     barrier = pltpu.get_barrier_semaphore()
-    for where in places:
+
+    def greet(where):
         pl.semaphore_signal(barrier, inc=1, device_id=where, device_id_type=MESH)
 
-    start_fetch(0, 0)
-    start_fetch(1, 0)
-    start_fetch(2, 0)
+    odd = lax.rem(gy, 2)
+    column = [(lax.rem(gy + 2 * k, ny), gx) for k in range(1, half)]
+    mates = [(gy, xs[d]) for d in order if d] + [(gy + 1 - 2 * odd, xs[d]) for d in order]
+    low_side, high_side = odd == 1, odd == 0
+    outside = [
+        (jnp.logical_and(low_side, down), (gy + 1, gx)),
+        (jnp.logical_and(low_side, jnp.logical_and(down, left)), (gy + 1, gx - 1)),
+        (jnp.logical_and(high_side, up), (gy - 1, gx)),
+        (jnp.logical_and(high_side, jnp.logical_and(up, right)), (gy - 1, gx + 1)),
+    ]
+    for where in column + mates:
+        greet(where)
+    guests = len(column) + len(mates)
+    for ok, where in outside:
+        guests = guests + jnp.where(ok, 1, 0)
+
+        @pl.when(ok)
+        def _(where=where):
+            greet(where)
 
     def later(g, c):
         start_fetch(1, g)
@@ -185,13 +206,19 @@
             def _(copy=copy):
                 copy.wait_send()
 
-    def send_message(slot, g, row):
+    def send_message(slot, g, row, chores):
         msg_send[slot, g] = row
         msg_recv[slot, g, me] = row
-        for where in places:
+        done = 0
+        for k, where in enumerate(places):
             remote(
                 msg_send.at[slot, g], msg_recv.at[slot, g, me], msg_ssem.at[slot, g], msg_rsem.at[slot, g], where
             ).start()
+            while done * len(places) < k * len(chores):
+                chores[done]()
+                done += 1
+        for chore in chores[done:]:
+            chore()
 
     def wait_message(slot, g):
         whole = msg_recv.at[slot, g, pl.ds(0, n - 1)]
@@ -245,7 +272,6 @@
         pack = pack_last(pack, CO[t][:, C - LANES:], t)
     cost_col[...] = pack
     cost_row[...] = line(cost_in, rows - 1)
-    lax.fori_loop(0, G, edges, 0)
 
     for missing, refs in (
         (jnp.logical_not(down), [row_recv.at[s, 0] for s in range(2)]),
@@ -265,14 +291,26 @@
         def _(ref=ref):
             ref[...] = jnp.ones(ref.shape, f32)
 
-    pl.semaphore_wait(barrier, n - 1)
-    start_all(prices())
+    edges(0, 0)
+    pl.semaphore_wait(barrier, guests)
+    for where in column:
+        pl.semaphore_signal(plane_sem, inc=1, device_id=where, device_id_type=MESH)
+    start_all(halos(0, 0) + extras(0) + prices())
 
     def announce(g, c):
+        edges(g, c)
         start_all(halos(0, g) + extras(g))
         return c
 
-    lax.fori_loop(0, G, announce, 0)
+    lax.fori_loop(1, G, announce, 0)
+
+    no_lane = jnp.zeros((SUBS, LANES), f32)
+
+    def above_first(a_last, ghost):
+        return jnp.where(subw == 0, row8(ghost), pltpu.roll(a_last, 1, 0))
+
+    def below_last(u_first):
+        return jnp.where(subw == SUBS - 1, 0.0, pltpu.roll(u_first, SUBS - 1, 0))
 
     def load(g, c):
         wait_fetch(3, g)
@@ -281,12 +319,16 @@
             B[g, t] = gather(flow_in, 1, g, t)
             U[g, t] = gather(u_in, g, t)
             IM[g, t] = gather(imb_in, g, t)
+        for t in range(T):
+            a, b, u = A[g, t], B[g, t], U[g, t]
+            above = A[g, t - 1] if t else above_first(A[g, T - 1], jnp.zeros((1, C), f32))
+            E[g, t] = ((a - above) + (b - to_right(b, no_lane))) + IM[g, t]
+            GA[g, t] = (U[g, t + 1] if t < T - 1 else below_last(U[g, 0])) - u
+            GB[g, t] = to_left(u, no_lane) - u
         return c
 
     lax.fori_loop(0, G, load, 0)
-
-    def above_first(a_last, ghost):
-        return jnp.where(subw == 0, row8(ghost), pltpu.roll(a_last, 1, 0))
+    pl.semaphore_wait(plane_sem, len(column))
 
     def divergence(t, a, above, b, gb):
         return ((a - above) + (b - to_right(b, turn_lanes(gb, -t))))
@@ -297,9 +339,9 @@
             grow[g, k] = ext_row_in[g, k]
             gcol[g, k] = ext_col_in[g, k]
         gb = gcol[g, 1]
+        E[g, 0] = E[g, 0] - jnp.where(subw == 0, row8(grow[g, 0]), 0.0)
         for t in range(T):
-            above = A[g, t - 1] if t else above_first(A[g, T - 1], grow[g, 0])
-            E[g, t] = divergence(t, A[g, t], above, B[g, t], gb) + IM[g, t]
+            E[g, t, :, :LANES] = E[g, t, :, :LANES] - jnp.where(lane == 0, turn_lanes(gb, -t), 0.0)
 
     def slopes(slot, g):
         wait_all(halos(slot, g))
@@ -315,17 +357,11 @@
         zero = jnp.zeros_like(u)
         slope_col[g, 0] = jnp.where(left, u_down - u, zero)
         slope_col[g, 1] = jnp.where(left, col_send[slot, 0, g] - u, zero)
-        below = row8(row_recv[slot, 0, g])
+        GA[g, T - 1] = GA[g, T - 1] + jnp.where(subw == SUBS - 1, row8(row_recv[slot, 0, g]), 0.0)
         beside = col_recv[slot, 0, g]
-        first = u = U[g, 0]
         for t in range(T):
-            if t < T - 1:
-                u_down = U[g, t + 1]
-            else:
-                u_down = jnp.where(subw == SUBS - 1, below, pltpu.roll(first, SUBS - 1, 0))
-            GA[g, t] = u_down - u
-            GB[g, t] = to_left(u, turn_lanes(beside, LANES - 1 - t)) - u
-            u = u_down
+            entering = jnp.where(lane == LANES - 1, turn_lanes(beside, LANES - 1 - t), 0.0)
+            GB[g, t, :, C - LANES:] = GB[g, t, :, C - LANES:] + entering
 
     def shrink(va, vb, t):
         f = jnp.maximum(1.0 - t * lax.rsqrt(va * va + vb * vb), 0.0)
@@ -333,17 +369,20 @@
 
     def adapt(slot, g):
         wait_message(slot, g)
-        primal, dual = (jnp.broadcast_to(v, (SUBS, LANES)) + epsilon for v in totals(slot, g))
+        sigma = sig_ref[g]
+        primal, dual = (jnp.broadcast_to(v, (SUBS, LANES)) for v in totals(slot, g))
+        primal = primal + epsilon
+        dual = sigma * sigma * dual + epsilon
         root = lax.rsqrt(primal) * (dual * lax.rsqrt(dual))
         s = lax.rsqrt(root)
         tau = tau_ref[g] * (root * s)
-        sigma = sig_ref[g] * s
+        sigma = sigma * s
         tau_ref[g] = tau
         sig_ref[g] = sigma
         return tau, sigma
 
-    def sweep(g, other, tau, sigma, closing):
-        wtau, wsigma = wide(tau), wide(sigma)
+    def sweep(g, other, tau, closing, chores):
+        wtau = wide(tau)
         tau1 = wtau[0:1]
         ghost_a, ghost_b = shrink(
             grow[g, 0] + tau1 * slope_row[g, 0], grow[g, 1] + tau1 * slope_row[g, 1], tau1 * cost_row_in[...]
@@ -361,14 +400,11 @@
         def dual(t, a2, above, b2):
             nonlocal acc_d
             q2 = divergence(t, a2, above, b2, side_b)
-            change = wsigma * ((q2 + q2) - E[g, t])
-            CH[g, t] = change
+            w = (q2 + q2) - E[g, t]
+            W[g, t] = w
             if closing:
-                miss = q2 - IM[g, t]
-                acc_d = acc_d + miss * miss
-            else:
-                Q[g, t] = q2
-                acc_d = acc_d + change * change
+                w = q2 - IM[g, t]
+            acc_d = acc_d + w * w
 
         for t in range(T):
             a, b = A[g, t], B[g, t]
@@ -387,23 +423,38 @@
                 a_first, b_first = a2, b2
             above = a2
         dual(0, a_first, above_first(above, ghost_a), b_first)
-        send_message(other, g, fold(acc_p, acc_d))
-
-    def settle(other, g):
+        send_message(other, g, fold(acc_p, acc_d), chores)
+
+    def settle(other, g, sigma):
         pack_f, pack_l = ones, ones
-        for t in range(T):
-            u2 = U[g, t] + CH[g, t]
+        first = prev = None
+        wsigma = wide(sigma)
+
+        def chore(t):
+            nonlocal pack_f, pack_l, first, prev
+            w = W[g, t]
+            u2 = U[g, t] + wsigma * w
             U[g, t] = u2
-            E[g, t] = Q[g, t] + IM[g, t]
+            E[g, t] = 0.5 * (w + E[g, t]) + IM[g, t]
+            GB[g, t] = to_left(u2, no_lane) - u2
             pack_f = pack_first(pack_f, u2[:, :LANES], t)
             pack_l = pack_last(pack_l, u2[:, C - LANES:], t)
             if t == 0:
                 row_send[other, 0, g] = u2[0:1]
+                first = u2
+            else:
+                GA[g, t - 1] = u2 - prev
             if t == T - 1:
                 row_send[other, 1, g] = u2[SUBS - 1:]
-        col_send[other, 0, g] = pack_f
-        col_send[other, 1, g] = pack_l
-        start_all(halos(other, g))
+                GA[g, t] = below_last(first) - u2
+            prev = u2
+
+        def leave():
+            col_send[other, 0, g] = pack_f
+            col_send[other, 1, g] = pack_l
+            start_all(halos(other, g))
+
+        return [functools.partial(chore, t) for t in range(T)], leave
 
     wait_all(prices())
 
@@ -413,8 +464,9 @@
         step = jnp.full((SUBS, LANES), initial_step, f32)
         tau_ref[g] = step
         sig_ref[g] = step
-        sweep(g, 1, step, step, False)
-        settle(1, g)
+        chores, leave = settle(1, g, step)
+        sweep(g, 1, step, False, chores)
+        leave()
         return c
 
     lax.fori_loop(0, G, opening, 0)
@@ -426,8 +478,9 @@
 
         def one(g, c):
             tau, sigma = adapt(slot, g)
-            sweep(g, other, tau, sigma, False)
-            settle(other, g)
+            chores, leave = settle(other, g, sigma)
+            sweep(g, other, tau, False, chores)
+            leave()
             slopes(jnp.where(g == G - 1, other, slot), lax.rem(g + 1, G))
             return c
 
@@ -438,14 +491,16 @@
 
     def close(g, c):
         tau, sigma = adapt(slot, g)
-        sweep(g, 1 - slot, tau, sigma, True)
+        wsigma = wide(sigma)
+
+        def chore(t):
+            scatter(u_in, U[g, t] + wsigma * W[g, t], g, t)
+
+        sweep(g, 1 - slot, tau, True, [functools.partial(chore, t) for t in range(T)])
 
         @pl.when(g < G - 1)
         def _():
             slopes(slot, g + 1)
-
-        for t in range(T):
-            scatter(u_in, U[g, t] + CH[g, t], g, t)
         return c
 
     lax.fori_loop(0, G, close, 0)
@@ -457,11 +512,33 @@
     for copy in results:
         copy.start()
     cells = T * SUBS * C * n
+    row = ones
     for g in range(G):
         wait_message(1 - slot, g)
-        res_out[g] = jnp.broadcast_to(totals(1 - slot, g)[1], (SUBS, LANES)) / cells
+        row = jnp.where(lane == g, totals(1 - slot, g)[1] / cells, row)
+    res_row[...] = row
+    results.append(pltpu.make_async_copy(res_row, res_out, out_sem.at[2, 0]))
+    results[-1].start()
     for copy in results:
         copy.wait()
+
+
+def finish(flow_in, u_in, res_in, flow_out, u_out, res_out, row, short, sems):
+    pairs = u_in.shape[0]
+    pick = pltpu.make_async_copy(res_in, row, sems.at[0, 0])
+    pick.start()
+    copies = [pltpu.make_async_copy(u_in.at[g], u_out.at[g], sems.at[1, g]) for g in range(pairs)] + [
+        pltpu.make_async_copy(flow_in.at[k, g], flow_out.at[k, g], sems.at[2 + k, g]) for k in range(2) for g in range(pairs)
+    ]
+    for copy in copies:
+        copy.start()
+    pick.wait()
+    short[...] = row[0:1, 0:pairs]
+    give = pltpu.make_async_copy(short, res_out, sems.at[0, 1])
+    give.start()
+    for copy in copies:
+        copy.wait()
+    give.wait()
 
 
 def local(ny, nx, imbalance, flow, potential, cost):
@@ -480,14 +557,14 @@
         out_shape=(
             jax.ShapeDtypeStruct(flow.shape, f32),
             jax.ShapeDtypeStruct(potential.shape, f32),
-            jax.ShapeDtypeStruct((G,) + packed, f32),
+            jax.ShapeDtypeStruct(packed, f32),
         ),
         in_specs=[hbm] * 4,
-        out_specs=(hbm, hbm, pl.BlockSpec(memory_space=pltpu.VMEM)),
+        out_specs=(hbm, hbm, hbm),
         scratch_shapes=[
             pltpu.VMEM((K, pairs, rows, LANES), f32), pltpu.VMEM((K, 2, pairs, rows, LANES), f32),
             pltpu.VMEM((K, pairs, rows, LANES), f32), pltpu.VMEM((K, rows, LANES), f32),
-        ] + [pltpu.VMEM(block, f32)] * 9 + [
+        ] + [pltpu.VMEM(block, f32)] * 8 + [
             pltpu.VMEM(block[1:], f32),
             pltpu.VMEM((G,) + packed, f32), pltpu.VMEM((G,) + packed, f32),
             pltpu.VMEM((2, 2, G, 1, cols), f32), pltpu.VMEM((2, 2, G) + packed, f32),
@@ -500,16 +577,29 @@
             pltpu.VMEM((1, cols), f32), pltpu.VMEM(packed, f32),
             pltpu.VMEM((G, 2, 1, cols), f32), pltpu.VMEM((G, 2) + packed, f32),
             pltpu.VMEM((G, 2, 1, cols), f32), pltpu.VMEM((G, 2) + packed, f32),
+            pltpu.VMEM(packed, f32),
             pltpu.SemaphoreType.DMA((2, 6, G)), pltpu.SemaphoreType.DMA((2, 6, G)),
             pltpu.SemaphoreType.DMA((2, G)), pltpu.SemaphoreType.DMA((2, G)),
             pltpu.SemaphoreType.DMA((2, G + 1)), pltpu.SemaphoreType.DMA((2, G + 1)),
-            pltpu.SemaphoreType.DMA((4, G, K)), pltpu.SemaphoreType.DMA((2, K)),
+            pltpu.SemaphoreType.DMA((4, G, K)), pltpu.SemaphoreType.DMA((3, K)), pltpu.SemaphoreType.REGULAR,
         ],
         compiler_params=pltpu.CompilerParams(
             collective_id=0, has_side_effects=True, vmem_limit_bytes=48 * 1024 * 1024
         ),
     )(*(pltpu.with_memory_space_constraint(x, pltpu.HBM) for x in (imbalance, flow, potential, cost)))
-    return flow_out, u_out, res[:, 0, 0]
+    anywhere = pl.BlockSpec(memory_space=pl.ANY)
+    flow_out, u_out, res = pl.pallas_call(
+        finish,
+        out_shape=(
+            jax.ShapeDtypeStruct(flow.shape, f32),
+            jax.ShapeDtypeStruct(potential.shape, f32),
+            jax.ShapeDtypeStruct((1, pairs), f32),
+        ),
+        in_specs=[anywhere] * 3,
+        out_specs=(hbm, hbm, hbm),
+        scratch_shapes=[pltpu.VMEM(packed, f32), pltpu.VMEM((1, pairs), f32), pltpu.SemaphoreType.DMA((4, max(pairs, 2)))],
+    )(*(pltpu.with_memory_space_constraint(x, pltpu.VMEM) for x in (flow_out, u_out, res)))
+    return flow_out, u_out, res.reshape(pairs)
 
 
 def solution(mesh):

time: 76.2 us -> 99.4 us (1.30)
  Pallas kernels: 72.5 us -> 98.6 us
  local copies, waits for them, and re-layouts: 2.91 us -> 0 us
    pallas_call x1, Pallas kernels: 72.5 us -> 96.8 us  [local(): pl.pallas_call(functools.partial(kernel, ny, nx), out_shape=(jax.ShapeDty...]
    unnamed x2 -> x0, local copies, waits for them, and re-layouts: 2.29 us -> none
    pallas_call x0 -> x1, Pallas kernels: none -> 1.8 us  [local(): pl.pallas_call(finish, out_shape=(jax.ShapeDtypeStruct(flow.shape, f32),...]
where the time goes in v2:
time: 99.4 us; the launch traced here: 99.3 us
  Pallas kernels  98.6 us (99%)
    pallas_call x1, Pallas kernels, local(): pl.pallas_call(functools.partial(kernel, ny, nx), out_shape=(jax.ShapeDty...  96.8 us

profile of v2, /device:TPU:0, one launch (start us, length us, event | category | flops | bytes accessed | tf_op | source)
XLA Modules:
  0.0 99.3 jit_solution(1803189635462358963)
XLA Ops:
  0.6 96.8 %shard_map.67 = (f32[2,4,128,512]{3,2,1,0:T(8,128)S(1)}, f32[4,128,512]{2,1,0:T(8,128)S(1)}, f32[8,128]{1,0:T(8,128)S(1)}) custom-call(f32[4,128,512]{2,1,0:T(8,128)} %imb_hbm.1, f32[2,4,128,512]{3,2,1,0:T(8,128)} %flow_hbm.1, f32[4,128,512]{2,1,0:T(8,128)} %u_hbm.1, f32[128,512]{1,0:T(8,128)} %cost_hbm.1), custom_call_target="tpu_custom_call" | custom-call | tf_op jit(solution)/shard_map/pallas_call | solution.py:555
  97.5 1.8 %shard_map.68 = (f32[2,4,128,512]{3,2,1,0:T(8,128)}, f32[4,128,512]{2,1,0:T(8,128)}, f32[1,4]{1,0:T(1,128)}) custom-call(f32[2,4,128,512]{3,2,1,0:T(8,128)S(1)} %get-tuple-element.9.flow_in, f32[4,128,512]{2,1,0:T(8,128)S(1)} %get-tuple-element.10.u_in, f32[8,128]{1,0:T(8,128)S(1)} %get-tuple-element.11.res_in), custom_call_target="tpu_custom_call" | custom-call | tf_op jit(solution)/shard_map/pallas_call | solution.py:591

commit v3 on v2

--- a/solution.py
+++ b/solution.py
@@ -1,4 +1,5 @@
 import functools
+import itertools
 
 import jax
 import jax.numpy as jnp
@@ -26,7 +27,7 @@
     row_send, col_send, row_recv, col_recv, corner_recv, msg_send, msg_recv,
     ext_row, ext_col, ext_row_in, ext_col_in, cost_row, cost_col, cost_row_in, cost_col_in,
     grow, gcol, slope_row, slope_col,
-    res_row,
+    res_row, spare,
     halo_ssem, halo_rsem, msg_ssem, msg_rsem, ext_ssem, ext_rsem, in_sem, out_sem, plane_sem,
 ):
     G, T, _, C = A.shape
@@ -41,24 +42,18 @@
     def piece(ref, k):
         return ref.at[(slice(None),) * (len(ref.shape) - 1) + (pl.ds(k * LANES, LANES),)]
 
-    def fetch(i, g, k):
-        if i == 0:
-            return pltpu.make_async_copy(piece(cost_hbm, k), cost_in.at[k], in_sem.at[0, 0, k])
-        if i == 1:
-            return pltpu.make_async_copy(piece(u_hbm.at[g], k), u_in.at[k, g], in_sem.at[1, g, k])
-        if i == 2:
-            return pltpu.make_async_copy(
-                flow_hbm.at[:, g, :, pl.ds(k * LANES, LANES)], flow_in.at[k, :, g], in_sem.at[2, g, k]
-            )
-        return pltpu.make_async_copy(piece(imb_hbm.at[g], k), imb_in.at[k, g], in_sem.at[3, g, k])
-
     def start_fetch(i, g):
         for k in range(K):
-            fetch(i, g, k).start()
+            at = pl.ds(k * LANES, LANES)
+            src, dst = (
+                (cost_hbm.at[:, at], cost_in.at[k]), (u_hbm.at[g, :, at], u_in.at[k, g]),
+                (flow_hbm.at[:, g, :, at], flow_in.at[k, :, g]), (imb_hbm.at[:, :, at], imb_in.at[k]),
+            )[i]
+            pltpu.make_async_copy(src, dst, in_sem.at[i, g]).start()
 
     def wait_fetch(i, g):
-        for k in range(K):
-            fetch(i, g, k).wait()
+        whole = (cost_in, u_in.at[:, g], flow_in.at[:, :, g], imb_in)[i]
+        pltpu.make_async_copy(whole, whole, in_sem.at[i, g]).wait()
 
     half = ny // 2
     low = gy < half
@@ -106,11 +101,7 @@
 
     lax.fori_loop(1, G, later, 0)
 
-    def last(g, c):
-        start_fetch(3, g)
-        return c
-
-    lax.fori_loop(0, G, last, 0)
+    start_fetch(3, 0)
 
     def gather(ref, *index):
         at = pl.ds(index[-1], SUBS, stride=T)
@@ -161,87 +152,92 @@
         )
 
     def halos(slot, g):
-        sems = lambda k: (halo_ssem.at[slot, k, g], halo_rsem.at[slot, k, g])
+        sems = (halo_ssem.at[g], halo_rsem.at[slot, g])
         head, tail = row_send.at[slot, 0, g], row_send.at[slot, 1, g]
         return [
-            (up, down, remote(head, row_recv.at[slot, 0, g], *sems(0), (gy - 1, gx))),
-            (down, up, remote(tail, row_recv.at[slot, 1, g], *sems(1), (gy + 1, gx))),
-            (left, right, remote(col_send.at[slot, 0, g], col_recv.at[slot, 0, g], *sems(2), (gy, gx - 1))),
-            (right, left, remote(col_send.at[slot, 1, g], col_recv.at[slot, 1, g], *sems(3), (gy, gx + 1))),
-            (
-                jnp.logical_and(down, left), jnp.logical_and(up, right),
-                remote(tail.at[:, pl.ds(0, LANES)], corner_recv.at[slot, 0, g], *sems(4), (gy + 1, gx - 1)),
-            ),
-            (
-                jnp.logical_and(up, right), jnp.logical_and(down, left),
-                remote(head.at[:, pl.ds(C - LANES, LANES)], corner_recv.at[slot, 1, g], *sems(5), (gy - 1, gx + 1)),
-            ),
+            (jnp.logical_and(down, left), remote(tail.at[:, pl.ds(0, LANES)], corner_recv.at[slot, 0, g], *sems, (gy + 1, gx - 1))),
+            (jnp.logical_and(up, right), remote(head.at[:, pl.ds(C - LANES, LANES)], corner_recv.at[slot, 1, g], *sems, (gy - 1, gx + 1))),
+            (up, remote(head, row_recv.at[slot, 0, g], *sems, (gy - 1, gx))),
+            (down, remote(tail, row_recv.at[slot, 1, g], *sems, (gy + 1, gx))),
+            (left, remote(col_send.at[slot, 0, g], col_recv.at[slot, 0, g], *sems, (gy, gx - 1))),
+            (right, remote(col_send.at[slot, 1, g], col_recv.at[slot, 1, g], *sems, (gy, gx + 1))),
         ]
 
     def extras(g):
+        sems = (ext_ssem.at[g], ext_rsem.at[g])
         return [
-            (down, up, remote(ext_row.at[g], ext_row_in.at[g], ext_ssem.at[0, g], ext_rsem.at[0, g], (gy + 1, gx))),
-            (right, left, remote(ext_col.at[g], ext_col_in.at[g], ext_ssem.at[1, g], ext_rsem.at[1, g], (gy, gx + 1))),
+            (down, remote(ext_row.at[g], ext_row_in.at[g], *sems, (gy + 1, gx))),
+            (right, remote(ext_col.at[g], ext_col_in.at[g], *sems, (gy, gx + 1))),
         ]
 
     def prices():
+        sems = (ext_ssem.at[G], ext_rsem.at[G])
         return [
-            (down, up, remote(cost_row, cost_row_in, ext_ssem.at[0, G], ext_rsem.at[0, G], (gy + 1, gx))),
-            (right, left, remote(cost_col, cost_col_in, ext_ssem.at[1, G], ext_rsem.at[1, G], (gy, gx + 1))),
+            (down, remote(cost_row, cost_row_in, *sems, (gy + 1, gx))),
+            (right, remote(cost_col, cost_col_in, *sems, (gy, gx + 1))),
         ]
 
     def start_all(copies):
-        for ok_to, _, copy in copies:
-            @pl.when(ok_to)
+        for ok, copy in copies:
+            @pl.when(ok)
             def _(copy=copy):
                 copy.start()
 
-    def wait_all(copies):
-        for ok_to, ok_from, copy in copies:
-            @pl.when(ok_from)
-            def _(copy=copy):
-                copy.wait_recv()
-
-            @pl.when(ok_to)
-            def _(copy=copy):
-                copy.wait_send()
-
-    def send_message(slot, g, row, chores):
-        msg_send[slot, g] = row
-        msg_recv[slot, g, me] = row
-        done = 0
-        for k, where in enumerate(places):
+    sides = [c for c in itertools.product((0, 1), repeat=4) if (c[0] or c[1]) and (c[2] or c[3])]
+
+    def lies(case):
+        flags = [f if has else jnp.logical_not(f) for f, has in zip((up, down, left, right), case)]
+        return functools.reduce(jnp.logical_and, flags)
+
+    def wait_rows(sem, count):
+        totals_of = {}
+        for case in sides:
+            totals_of.setdefault(count(*case), []).append(case)
+        for total, cases in totals_of.items():
+            if total:
+                @pl.when(functools.reduce(jnp.logical_or, [lies(case) for case in cases]))
+                def _(total=total):
+                    whole = spare.at[pl.ds(0, total)]
+                    pltpu.make_async_copy(whole, whole, sem).wait()
+
+    def wait_halos(slot, g):
+        count = lambda u, d, l, r: K * (u + d) + SUBS * (l + r) + u * r + d * l
+        wait_rows(halo_rsem.at[slot, g], count)
+        wait_rows(halo_ssem.at[g], count)
+
+    def wait_edges(k, parts):
+        wait_rows(ext_rsem.at[k], lambda u, d, l, r: parts * (K * u + SUBS * l))
+        wait_rows(ext_ssem.at[k], lambda u, d, l, r: parts * (K * d + SUBS * r))
+
+    def send_message(slot, g, rows, chores):
+        for k, row in enumerate(rows):
+            msg_send[slot, g, k:k + 1] = row
+            msg_recv[slot, g, me, k:k + 1] = row
+        for where in places:
             remote(
-                msg_send.at[slot, g], msg_recv.at[slot, g, me], msg_ssem.at[slot, g], msg_rsem.at[slot, g], where
+                msg_send.at[slot, g], msg_recv.at[slot, g, me], msg_ssem.at[g], msg_rsem.at[slot, g], where
             ).start()
-            while done * len(places) < k * len(chores):
-                chores[done]()
-                done += 1
-        for chore in chores[done:]:
+        for chore in chores:
             chore()
 
     def wait_message(slot, g):
         whole = msg_recv.at[slot, g, pl.ds(0, n - 1)]
         pltpu.make_async_copy(whole, whole, msg_rsem.at[slot, g]).wait()
-        pltpu.make_async_copy(whole, whole, msg_ssem.at[slot, g]).wait()
+        pltpu.make_async_copy(whole, whole, msg_ssem.at[g]).wait()
 
     def totals(slot, g):
         parts = [msg_recv[slot, g, k] for k in range(n)]
         while len(parts) > 1:
             parts = [sum(parts[k + 1:k + 2], parts[k]) for k in range(0, len(parts), 2)]
-        both = row8(parts[0])
-        first = lane < LANES // 2
-        return [
-            jnp.sum(jnp.where(keep, both, 0.0), axis=1, keepdims=True) for keep in (first, jnp.logical_not(first))
-        ]
+        return [jnp.sum(row8(parts[0][k:k + 1]), axis=1, keepdims=True) for k in range(2)]
 
     def fold(x, y):
         x, y = (sum((v[:, k * LANES:(k + 1) * LANES] for k in range(1, K)), v[:, :LANES]) for v in (x, y))
-        first = lane < LANES // 2
-        z = jnp.where(first, x, y) + pltpu.roll(jnp.where(first, y, x), LANES // 2, 1)
-        for step in (4, 2, 1):
-            z = z + pltpu.roll(z, step, 0)
-        return z[0:1]
+        half = SUBS // 2
+        z = jnp.where(sub < half, x + pltpu.roll(x, half, 0), y + pltpu.roll(y, half, 0))
+        z = z + pltpu.roll(z, 1, 0)
+        z = z + pltpu.roll(z, 2, 0)
+        return z[half - 1:half], z[SUBS - 1:]
 
 
     def edges(g, c):
@@ -312,8 +308,9 @@
     def below_last(u_first):
         return jnp.where(subw == SUBS - 1, 0.0, pltpu.roll(u_first, SUBS - 1, 0))
 
+    wait_fetch(3, 0)
+
     def load(g, c):
-        wait_fetch(3, g)
         for t in range(T):
             A[g, t] = gather(flow_in, 0, g, t)
             B[g, t] = gather(flow_in, 1, g, t)
@@ -334,7 +331,7 @@
         return ((a - above) + (b - to_right(b, turn_lanes(gb, -t))))
 
     def begin(g):
-        wait_all(extras(g))
+        wait_edges(g, 2)
         for k in range(2):
             grow[g, k] = ext_row_in[g, k]
             gcol[g, k] = ext_col_in[g, k]
@@ -344,7 +341,7 @@
             E[g, t, :, :LANES] = E[g, t, :, :LANES] - jnp.where(lane == 0, turn_lanes(gb, -t), 0.0)
 
     def slopes(slot, g):
-        wait_all(halos(slot, g))
+        wait_halos(slot, g)
         u = row_recv[slot, 1, g]
         u_right = to_left(u, turn_lanes(corner_recv[slot, 0, g], LANES - 1))
         zero = jnp.zeros_like(u)
@@ -456,7 +453,7 @@
 
         return [functools.partial(chore, t) for t in range(T)], leave
 
-    wait_all(prices())
+    wait_edges(G, 1)
 
     def opening(g, c):
         begin(g)
@@ -505,7 +502,7 @@
 
     lax.fori_loop(0, G, close, 0)
     results = [
-        pltpu.make_async_copy(src.at[k], piece(dst, k), out_sem.at[i, k])
+        pltpu.make_async_copy(src.at[k], piece(dst, k), out_sem.at[i])
         for i, (src, dst) in enumerate(((flow_in, flow_hbm_out), (u_in, u_hbm_out)))
         for k in range(K)
     ]
@@ -517,24 +514,22 @@
         wait_message(1 - slot, g)
         row = jnp.where(lane == g, totals(1 - slot, g)[1] / cells, row)
     res_row[...] = row
-    results.append(pltpu.make_async_copy(res_row, res_out, out_sem.at[2, 0]))
-    results[-1].start()
-    for copy in results:
-        copy.wait()
+    give = pltpu.make_async_copy(res_row, res_out, out_sem.at[2])
+    give.start()
+    for i, whole in enumerate((flow_hbm_out, u_hbm_out)):
+        pltpu.make_async_copy(whole, whole, out_sem.at[i]).wait()
+    give.wait()
 
 
 def finish(flow_in, u_in, res_in, flow_out, u_out, res_out, row, short, sems):
-    pairs = u_in.shape[0]
-    pick = pltpu.make_async_copy(res_in, row, sems.at[0, 0])
+    pick = pltpu.make_async_copy(res_in, row, sems.at[0])
     pick.start()
-    copies = [pltpu.make_async_copy(u_in.at[g], u_out.at[g], sems.at[1, g]) for g in range(pairs)] + [
-        pltpu.make_async_copy(flow_in.at[k, g], flow_out.at[k, g], sems.at[2 + k, g]) for k in range(2) for g in range(pairs)
-    ]
+    copies = [pltpu.make_async_copy(u_in, u_out, sems.at[1]), pltpu.make_async_copy(flow_in, flow_out, sems.at[2])]
     for copy in copies:
         copy.start()
     pick.wait()
-    short[...] = row[0:1, 0:pairs]
-    give = pltpu.make_async_copy(short, res_out, sems.at[0, 1])
+    short[...] = row[0:1, 0:short.shape[1]]
+    give = pltpu.make_async_copy(short, res_out, sems.at[0])
     give.start()
     for copy in copies:
         copy.wait()
@@ -545,7 +540,8 @@
     pairs, rows, cols = imbalance.shape
     T = rows // SUBS
     n = ny * nx
-    assert rows % SUBS == 0 and cols % LANES == 0 and 4 <= T <= LANES and ny % 2 == 0
+    assert rows % SUBS == 0 and cols % LANES == 0 and 4 <= T < LANES and ny % 2 == 0 and nx > 1
+    assert pairs <= LANES
     G = pairs
     f32 = jnp.float32
     block = (pairs, T, SUBS, cols)
@@ -570,18 +566,18 @@
             pltpu.VMEM((2, 2, G, 1, cols), f32), pltpu.VMEM((2, 2, G) + packed, f32),
             pltpu.VMEM((2, 2, G, 1, cols), f32), pltpu.VMEM((2, 2, G) + packed, f32),
             pltpu.VMEM((2, 2, G, 1, LANES), f32),
-            pltpu.VMEM((2, G, 1, LANES), f32), pltpu.VMEM((2, G, n, 1, LANES), f32),
+            pltpu.VMEM((2, G, 2, LANES), f32), pltpu.VMEM((2, G, n, 2, LANES), f32),
             pltpu.VMEM((G, 2, 1, cols), f32), pltpu.VMEM((G, 2) + packed, f32),
             pltpu.VMEM((G, 2, 1, cols), f32), pltpu.VMEM((G, 2) + packed, f32),
             pltpu.VMEM((1, cols), f32), pltpu.VMEM(packed, f32),
             pltpu.VMEM((1, cols), f32), pltpu.VMEM(packed, f32),
             pltpu.VMEM((G, 2, 1, cols), f32), pltpu.VMEM((G, 2) + packed, f32),
             pltpu.VMEM((G, 2, 1, cols), f32), pltpu.VMEM((G, 2) + packed, f32),
-            pltpu.VMEM(packed, f32),
-            pltpu.SemaphoreType.DMA((2, 6, G)), pltpu.SemaphoreType.DMA((2, 6, G)),
-            pltpu.SemaphoreType.DMA((2, G)), pltpu.SemaphoreType.DMA((2, G)),
-            pltpu.SemaphoreType.DMA((2, G + 1)), pltpu.SemaphoreType.DMA((2, G + 1)),
-            pltpu.SemaphoreType.DMA((4, G, K)), pltpu.SemaphoreType.DMA((3, K)), pltpu.SemaphoreType.REGULAR,
+            pltpu.VMEM(packed, f32), pltpu.VMEM((2 * K + 2 * SUBS + 2, 1, LANES), f32),
+            pltpu.SemaphoreType.DMA((G,)), pltpu.SemaphoreType.DMA((2, G)),
+            pltpu.SemaphoreType.DMA((G,)), pltpu.SemaphoreType.DMA((2, G)),
+            pltpu.SemaphoreType.DMA((G + 1,)), pltpu.SemaphoreType.DMA((G + 1,)),
+            pltpu.SemaphoreType.DMA((4, G)), pltpu.SemaphoreType.DMA((3,)), pltpu.SemaphoreType.REGULAR,
         ],
         compiler_params=pltpu.CompilerParams(
             collective_id=0, has_side_effects=True, vmem_limit_bytes=48 * 1024 * 1024
@@ -597,7 +593,7 @@
         ),
         in_specs=[anywhere] * 3,
         out_specs=(hbm, hbm, hbm),
-        scratch_shapes=[pltpu.VMEM(packed, f32), pltpu.VMEM((1, pairs), f32), pltpu.SemaphoreType.DMA((4, max(pairs, 2)))],
+        scratch_shapes=[pltpu.VMEM(packed, f32), pltpu.VMEM((1, pairs), f32), pltpu.SemaphoreType.DMA((3,))],
     )(*(pltpu.with_memory_space_constraint(x, pltpu.VMEM) for x in (flow_out, u_out, res)))
     return flow_out, u_out, res.reshape(pairs)
 

time: 99.4 us -> 71.7 us (0.72)
  Pallas kernels: 98.6 us -> 70.9 us
    pallas_call x1, Pallas kernels: 96.8 us -> 69.2 us  [local(): pl.pallas_call(functools.partial(kernel, ny, nx), out_shape=(jax.ShapeDty...]
where the time goes in v3:
time: 71.7 us; the launch traced here: 71.5 us
  Pallas kernels  70.9 us (99%)
    pallas_call x1, Pallas kernels, local(): pl.pallas_call(functools.partial(kernel, ny, nx), out_shape=(jax.ShapeDty...  69.2 us
    pallas_call x1, Pallas kernels, local(): pl.pallas_call(finish, out_shape=(jax.ShapeDtypeStruct(flow.shape, f32),...  1.7 us

profile of v3, /device:TPU:0, one launch (start us, length us, event | category | flops | bytes accessed | tf_op | source)
XLA Modules:
  0.0 71.5 jit_solution(17885748397218252228)
XLA Ops:
  0.6 69.2 %shard_map.67 = (f32[2,4,128,512]{3,2,1,0:T(8,128)S(1)}, f32[4,128,512]{2,1,0:T(8,128)S(1)}, f32[8,128]{1,0:T(8,128)S(1)}) custom-call(f32[4,128,512]{2,1,0:T(8,128)} %imb_hbm.1, f32[2,4,128,512]{3,2,1,0:T(8,128)} %flow_hbm.1, f32[4,128,512]{2,1,0:T(8,128)} %u_hbm.1, f32[128,512]{1,0:T(8,128)} %cost_hbm.1), custom_call_target="tpu_custom_call" | custom-call | tf_op jit(solution)/shard_map/pallas_call | solution.py:551
  69.8 1.7 %shard_map.68 = (f32[2,4,128,512]{3,2,1,0:T(8,128)}, f32[4,128,512]{2,1,0:T(8,128)}, f32[1,4]{1,0:T(1,128)}) custom-call(f32[2,4,128,512]{3,2,1,0:T(8,128)S(1)} %get-tuple-element.9.flow_in, f32[4,128,512]{2,1,0:T(8,128)S(1)} %get-tuple-element.10.u_in, f32[8,128]{1,0:T(8,128)S(1)} %get-tuple-element.11.res_in), custom_call_target="tpu_custom_call" | custom-call | tf_op jit(solution)/shard_map/pallas_call | solution.py:587

commit v4 on v3

--- a/solution.py
+++ b/solution.py
@@ -28,7 +28,7 @@
     ext_row, ext_col, ext_row_in, ext_col_in, cost_row, cost_col, cost_row_in, cost_col_in,
     grow, gcol, slope_row, slope_col,
     res_row, spare,
-    halo_ssem, halo_rsem, msg_ssem, msg_rsem, ext_ssem, ext_rsem, in_sem, out_sem, plane_sem,
+    halo_ssem, halo_rsem, msg_ssem, msg_rsem, out_sem, plane_sem,
 ):
     G, T, _, C = A.shape
     n = ny * nx
@@ -42,6 +42,9 @@
     def piece(ref, k):
         return ref.at[(slice(None),) * (len(ref.shape) - 1) + (pl.ds(k * LANES, LANES),)]
 
+    def fetch_sem(i, g):
+        return (out_sem.at[1], msg_ssem.at[g], halo_ssem.at[g], out_sem.at[0])[i]
+
     def start_fetch(i, g):
         for k in range(K):
             at = pl.ds(k * LANES, LANES)
@@ -49,11 +52,11 @@
                 (cost_hbm.at[:, at], cost_in.at[k]), (u_hbm.at[g, :, at], u_in.at[k, g]),
                 (flow_hbm.at[:, g, :, at], flow_in.at[k, :, g]), (imb_hbm.at[:, :, at], imb_in.at[k]),
             )[i]
-            pltpu.make_async_copy(src, dst, in_sem.at[i, g]).start()
+            pltpu.make_async_copy(src, dst, fetch_sem(i, g)).start()
 
     def wait_fetch(i, g):
         whole = (cost_in, u_in.at[:, g], flow_in.at[:, :, g], imb_in)[i]
-        pltpu.make_async_copy(whole, whole, in_sem.at[i, g]).wait()
+        pltpu.make_async_copy(whole, whole, fetch_sem(i, g)).wait()
 
     half = ny // 2
     low = gy < half
@@ -67,8 +70,8 @@
     places += [(gy, xs[d]) for d in order if d]
 
     start_fetch(1, 0)
+    start_fetch(2, 0)
     start_fetch(0, 0)
-    start_fetch(2, 0)
     barrier = pltpu.get_barrier_semaphore()
 
     def greet(where):
@@ -164,14 +167,14 @@
         ]
 
     def extras(g):
-        sems = (ext_ssem.at[g], ext_rsem.at[g])
+        sems = (msg_ssem.at[g], msg_rsem.at[0, g])
         return [
             (down, remote(ext_row.at[g], ext_row_in.at[g], *sems, (gy + 1, gx))),
             (right, remote(ext_col.at[g], ext_col_in.at[g], *sems, (gy, gx + 1))),
         ]
 
     def prices():
-        sems = (ext_ssem.at[G], ext_rsem.at[G])
+        sems = (out_sem.at[1], out_sem.at[2])
         return [
             (down, remote(cost_row, cost_row_in, *sems, (gy + 1, gx))),
             (right, remote(cost_col, cost_col_in, *sems, (gy, gx + 1))),
@@ -205,11 +208,11 @@
         wait_rows(halo_rsem.at[slot, g], count)
         wait_rows(halo_ssem.at[g], count)
 
-    def wait_edges(k, parts):
-        wait_rows(ext_rsem.at[k], lambda u, d, l, r: parts * (K * u + SUBS * l))
-        wait_rows(ext_ssem.at[k], lambda u, d, l, r: parts * (K * d + SUBS * r))
-
-    def send_message(slot, g, rows, chores):
+    def wait_edges(ssem, rsem, parts):
+        wait_rows(rsem, lambda u, d, l, r: parts * (K * u + SUBS * l))
+        wait_rows(ssem, lambda u, d, l, r: parts * (K * d + SUBS * r))
+
+    def send_message(slot, g, rows):
         for k, row in enumerate(rows):
             msg_send[slot, g, k:k + 1] = row
             msg_recv[slot, g, me, k:k + 1] = row
@@ -217,8 +220,6 @@
             remote(
                 msg_send.at[slot, g], msg_recv.at[slot, g, me], msg_ssem.at[g], msg_rsem.at[slot, g], where
             ).start()
-        for chore in chores:
-            chore()
 
     def wait_message(slot, g):
         whole = msg_recv.at[slot, g, pl.ds(0, n - 1)]
@@ -260,14 +261,6 @@
             ext_col[g, k] = packs[2 + k]
             ext_row[g, k] = line(flow_in, k, g, rows - 1)
         return c
-
-    wait_fetch(0, 0)
-    pack = ones
-    for t in range(T):
-        CO[t] = gather(cost_in, t)
-        pack = pack_last(pack, CO[t][:, C - LANES:], t)
-    cost_col[...] = pack
-    cost_row[...] = line(cost_in, rows - 1)
 
     for missing, refs in (
         (jnp.logical_not(down), [row_recv.at[s, 0] for s in range(2)]),
@@ -291,7 +284,15 @@
     pl.semaphore_wait(barrier, guests)
     for where in column:
         pl.semaphore_signal(plane_sem, inc=1, device_id=where, device_id_type=MESH)
-    start_all(halos(0, 0) + extras(0) + prices())
+    start_all(halos(0, 0) + extras(0))
+    wait_fetch(0, 0)
+    pack = ones
+    for t in range(T):
+        CO[t] = gather(cost_in, t)
+        pack = pack_last(pack, CO[t][:, C - LANES:], t)
+    cost_col[...] = pack
+    cost_row[...] = line(cost_in, rows - 1)
+    start_all(prices())
 
     def announce(g, c):
         edges(g, c)
@@ -331,7 +332,7 @@
         return ((a - above) + (b - to_right(b, turn_lanes(gb, -t))))
 
     def begin(g):
-        wait_edges(g, 2)
+        wait_edges(msg_ssem.at[g], msg_rsem.at[0, g], 2)
         for k in range(2):
             grow[g, k] = ext_row_in[g, k]
             gcol[g, k] = ext_col_in[g, k]
@@ -378,7 +379,7 @@
         sig_ref[g] = sigma
         return tau, sigma
 
-    def sweep(g, other, tau, closing, chores):
+    def sweep(g, other, tau, closing):
         wtau = wide(tau)
         tau1 = wtau[0:1]
         ghost_a, ghost_b = shrink(
@@ -406,12 +407,9 @@
         for t in range(T):
             a, b = A[g, t], B[g, t]
             a2, b2 = shrink(a + wtau * GA[g, t], b + wtau * GB[g, t], wtau * CO[t])
-            if closing:
-                scatter(flow_in, a2, 0, g, t)
-                scatter(flow_in, b2, 1, g, t)
-            else:
-                A[g, t] = a2
-                B[g, t] = b2
+            A[g, t] = a2
+            B[g, t] = b2
+            if not closing:
                 da, db = a2 - a, b2 - b
                 acc_p = acc_p + (da * da + db * db)
             if t:
@@ -420,40 +418,55 @@
                 a_first, b_first = a2, b2
             above = a2
         dual(0, a_first, above_first(above, ghost_a), b_first)
-        send_message(other, g, fold(acc_p, acc_d), chores)
-
-    def settle(other, g, sigma):
-        pack_f, pack_l = ones, ones
-        first = prev = None
-        wsigma = wide(sigma)
-
-        def chore(t):
-            nonlocal pack_f, pack_l, first, prev
+        send_message(other, g, fold(acc_p, acc_d))
+
+    ends = sorted({0, K - 1})
+
+    def chunk(k):
+        return pl.ds(k * LANES, LANES)
+
+    def depart(other, g, sigma):
+        packs = [ones, ones]
+        for t in range(T):
+            for k in range(K) if t in (0, T - 1) else ends:
+                u2 = U[g, t, :, chunk(k)] + sigma * W[g, t, :, chunk(k)]
+                U[g, t, :, chunk(k)] = u2
+                if k == 0:
+                    packs[0] = pack_first(packs[0], u2, t)
+                if k == K - 1:
+                    packs[1] = pack_last(packs[1], u2, t)
+                if t == 0:
+                    row_send[other, 0, g, :, chunk(k)] = u2[0:1]
+                if t == T - 1:
+                    row_send[other, 1, g, :, chunk(k)] = u2[SUBS - 1:]
+        for k in range(2):
+            col_send[other, k, g] = packs[k]
+        start_all(halos(other, g))
+
+    def settle(g, c):
+        sigma = sig_ref[g]
+        first = prev = U[g, 0]
+        for t in range(T):
             w = W[g, t]
-            u2 = U[g, t] + wsigma * w
-            U[g, t] = u2
             E[g, t] = 0.5 * (w + E[g, t]) + IM[g, t]
+            if t in (0, T - 1):
+                u2 = U[g, t]
+            else:
+                inner = [
+                    U[g, t, :, chunk(k)] if k in ends else U[g, t, :, chunk(k)] + sigma * w[:, k * LANES:(k + 1) * LANES]
+                    for k in range(K)
+                ]
+                for k in range(K):
+                    if k not in ends:
+                        U[g, t, :, chunk(k)] = inner[k]
+                u2 = jnp.concatenate(inner, axis=1)
             GB[g, t] = to_left(u2, no_lane) - u2
-            pack_f = pack_first(pack_f, u2[:, :LANES], t)
-            pack_l = pack_last(pack_l, u2[:, C - LANES:], t)
-            if t == 0:
-                row_send[other, 0, g] = u2[0:1]
-                first = u2
-            else:
+            if t:
                 GA[g, t - 1] = u2 - prev
             if t == T - 1:
-                row_send[other, 1, g] = u2[SUBS - 1:]
                 GA[g, t] = below_last(first) - u2
             prev = u2
-
-        def leave():
-            col_send[other, 0, g] = pack_f
-            col_send[other, 1, g] = pack_l
-            start_all(halos(other, g))
-
-        return [functools.partial(chore, t) for t in range(T)], leave
-
-    wait_edges(G, 1)
+        return c
 
     def opening(g, c):
         begin(g)
@@ -461,12 +474,16 @@
         step = jnp.full((SUBS, LANES), initial_step, f32)
         tau_ref[g] = step
         sig_ref[g] = step
-        chores, leave = settle(1, g, step)
-        sweep(g, 1, step, False, chores)
-        leave()
+        @pl.when(g == 0)
+        def _():
+            wait_edges(out_sem.at[1], out_sem.at[2], 1)
+
+        sweep(g, 1, step, False)
+        depart(1, g, step)
         return c
 
     lax.fori_loop(0, G, opening, 0)
+    lax.fori_loop(0, G, settle, 0)
     slopes(1, 0)
 
     def turn(i, c):
@@ -475,32 +492,42 @@
 
         def one(g, c):
             tau, sigma = adapt(slot, g)
-            chores, leave = settle(other, g, sigma)
-            sweep(g, other, tau, False, chores)
-            leave()
-            slopes(jnp.where(g == G - 1, other, slot), lax.rem(g + 1, G))
+            sweep(g, other, tau, False)
+            depart(other, g, sigma)
+
+            @pl.when(g < G - 1)
+            def _():
+                slopes(slot, g + 1)
+
             return c
 
-        return lax.fori_loop(0, G, one, c)
+        lax.fori_loop(0, G, one, c)
+        lax.fori_loop(0, G, settle, c)
+        slopes(other, 0)
+        return c
 
     lax.fori_loop(1, ITERS - 1, turn, 0)
     slot = (ITERS - 1) % 2
 
     def close(g, c):
-        tau, sigma = adapt(slot, g)
-        wsigma = wide(sigma)
-
-        def chore(t):
-            scatter(u_in, U[g, t] + wsigma * W[g, t], g, t)
-
-        sweep(g, 1 - slot, tau, True, [functools.partial(chore, t) for t in range(T)])
+        sweep(g, 1 - slot, adapt(slot, g)[0], True)
 
         @pl.when(g < G - 1)
         def _():
             slopes(slot, g + 1)
+
+        return c
+
+    def unload(g, c):
+        wsigma = wide(sig_ref[g])
+        for t in range(T):
+            scatter(flow_in, A[g, t], 0, g, t)
+            scatter(flow_in, B[g, t], 1, g, t)
+            scatter(u_in, U[g, t] + wsigma * W[g, t], g, t)
         return c
 
     lax.fori_loop(0, G, close, 0)
+    lax.fori_loop(0, G, unload, 0)
     results = [
         pltpu.make_async_copy(src.at[k], piece(dst, k), out_sem.at[i])
         for i, (src, dst) in enumerate(((flow_in, flow_hbm_out), (u_in, u_hbm_out)))
@@ -576,8 +603,7 @@
             pltpu.VMEM(packed, f32), pltpu.VMEM((2 * K + 2 * SUBS + 2, 1, LANES), f32),
             pltpu.SemaphoreType.DMA((G,)), pltpu.SemaphoreType.DMA((2, G)),
             pltpu.SemaphoreType.DMA((G,)), pltpu.SemaphoreType.DMA((2, G)),
-            pltpu.SemaphoreType.DMA((G + 1,)), pltpu.SemaphoreType.DMA((G + 1,)),
-            pltpu.SemaphoreType.DMA((4, G)), pltpu.SemaphoreType.DMA((3,)), pltpu.SemaphoreType.REGULAR,
+            pltpu.SemaphoreType.DMA((3,)), pltpu.SemaphoreType.REGULAR,
         ],
         compiler_params=pltpu.CompilerParams(
             collective_id=0, has_side_effects=True, vmem_limit_bytes=48 * 1024 * 1024

time: 71.7 us -> 71 us (level)
  no operation moved by 1% of the time
where the time goes in v4:
time: 71 us; the launch traced here: 70.9 us
  Pallas kernels  70.2 us (99%)
    pallas_call x1, Pallas kernels, local(): pl.pallas_call(functools.partial(kernel, ny, nx), out_shape=(jax.ShapeDty...  68.5 us
    pallas_call x1, Pallas kernels, local(): pl.pallas_call(finish, out_shape=(jax.ShapeDtypeStruct(flow.shape, f32),...  1.7 us

profile of v4, /device:TPU:0, one launch (start us, length us, event | category | flops | bytes accessed | tf_op | source)
XLA Modules:
  0.0 70.9 jit_solution(14870843834421952284)
XLA Ops:
  0.6 68.5 %shard_map.67 = (f32[2,4,128,512]{3,2,1,0:T(8,128)S(1)}, f32[4,128,512]{2,1,0:T(8,128)S(1)}, f32[8,128]{1,0:T(8,128)S(1)}) custom-call(f32[4,128,512]{2,1,0:T(8,128)} %imb_hbm.1, f32[2,4,128,512]{3,2,1,0:T(8,128)} %flow_hbm.1, f32[4,128,512]{2,1,0:T(8,128)} %u_hbm.1, f32[128,512]{1,0:T(8,128)} %cost_hbm.1), custom_call_target="tpu_custom_call" | custom-call | tf_op jit(solution)/shard_map/pallas_call | solution.py:578
  69.2 1.7 %shard_map.68 = (f32[2,4,128,512]{3,2,1,0:T(8,128)}, f32[4,128,512]{2,1,0:T(8,128)}, f32[1,4]{1,0:T(1,128)}) custom-call(f32[2,4,128,512]{3,2,1,0:T(8,128)S(1)} %get-tuple-element.9.flow_in, f32[4,128,512]{2,1,0:T(8,128)S(1)} %get-tuple-element.10.u_in, f32[8,128]{1,0:T(8,128)S(1)} %get-tuple-element.11.res_in), custom_call_target="tpu_custom_call" | custom-call | tf_op jit(solution)/shard_map/pallas_call | solution.py:613

commit v5 on v4

--- a/solution.py
+++ b/solution.py
@@ -62,8 +62,9 @@
     low = gy < half
     xs = [lax.rem(gx + d, nx) for d in range(nx)]
     order = sorted(range(nx), key=lambda d: -min(d, nx - d))
-    places = [(jnp.where(low, ny - 1 - j, j), xs[d]) for j in range(half) for d in order]
     high = jnp.where(low, ny - 1 - gy, gy) - half
+    across = [half + lax.rem(high + half - j, half) for j in range(half)]
+    places = [(jnp.where(low, y, ny - 1 - y), xs[d]) for y in across for d in order]
     for k in range(1, ny - half):
         y = half + lax.rem(high + k, ny - half)
         places += [(jnp.where(low, ny - 1 - y, y), xs[d]) for d in order]
@@ -304,7 +305,7 @@
     no_lane = jnp.zeros((SUBS, LANES), f32)
 
     def above_first(a_last, ghost):
-        return jnp.where(subw == 0, row8(ghost), pltpu.roll(a_last, 1, 0))
+        return jnp.where(subw == 0, ghost, pltpu.roll(a_last, 1, 0))
 
     def below_last(u_first):
         return jnp.where(subw == SUBS - 1, 0.0, pltpu.roll(u_first, SUBS - 1, 0))
@@ -319,7 +320,7 @@
             IM[g, t] = gather(imb_in, g, t)
         for t in range(T):
             a, b, u = A[g, t], B[g, t], U[g, t]
-            above = A[g, t - 1] if t else above_first(A[g, T - 1], jnp.zeros((1, C), f32))
+            above = A[g, t - 1] if t else above_first(A[g, T - 1], 0.0)
             E[g, t] = ((a - above) + (b - to_right(b, no_lane))) + IM[g, t]
             GA[g, t] = (U[g, t + 1] if t < T - 1 else below_last(U[g, 0])) - u
             GB[g, t] = to_left(u, no_lane) - u
@@ -334,19 +335,19 @@
     def begin(g):
         wait_edges(msg_ssem.at[g], msg_rsem.at[0, g], 2)
         for k in range(2):
-            grow[g, k] = ext_row_in[g, k]
+            grow[g, k] = row8(ext_row_in[g, k])
             gcol[g, k] = ext_col_in[g, k]
         gb = gcol[g, 1]
-        E[g, 0] = E[g, 0] - jnp.where(subw == 0, row8(grow[g, 0]), 0.0)
+        E[g, 0] = E[g, 0] - jnp.where(subw == 0, grow[g, 0], 0.0)
         for t in range(T):
             E[g, t, :, :LANES] = E[g, t, :, :LANES] - jnp.where(lane == 0, turn_lanes(gb, -t), 0.0)
 
     def slopes(slot, g):
         wait_halos(slot, g)
-        u = row_recv[slot, 1, g]
-        u_right = to_left(u, turn_lanes(corner_recv[slot, 0, g], LANES - 1))
+        u = row8(row_recv[slot, 1, g])
+        u_right = to_left(u, row8(turn_lanes(corner_recv[slot, 0, g], LANES - 1)))
         zero = jnp.zeros_like(u)
-        slope_row[g, 0] = jnp.where(up, row_send[slot, 0, g] - u, zero)
+        slope_row[g, 0] = jnp.where(up, row8(row_send[slot, 0, g]) - u, zero)
         slope_row[g, 1] = jnp.where(up, u_right - u, zero)
         u = col_recv[slot, 1, g]
         turn = turn_lanes(pltpu.roll(u, SUBS - 1, 0), T - 1)
@@ -361,32 +362,31 @@
             entering = jnp.where(lane == LANES - 1, turn_lanes(beside, LANES - 1 - t), 0.0)
             GB[g, t, :, C - LANES:] = GB[g, t, :, C - LANES:] + entering
 
-    def shrink(va, vb, t):
-        f = jnp.maximum(1.0 - t * lax.rsqrt(va * va + vb * vb), 0.0)
+    def shrink(va, vb, c):
+        f = jnp.maximum(1.0 - c * lax.rsqrt(va * va + vb * vb), 0.0)
         return f * va, f * vb
 
     def adapt(slot, g):
+        tau, sigma = tau_ref[g], sig_ref[g]
         wait_message(slot, g)
-        sigma = sig_ref[g]
         primal, dual = (jnp.broadcast_to(v, (SUBS, LANES)) for v in totals(slot, g))
-        primal = primal + epsilon
+        primal = tau * tau * primal + epsilon
         dual = sigma * sigma * dual + epsilon
         root = lax.rsqrt(primal) * (dual * lax.rsqrt(dual))
         s = lax.rsqrt(root)
-        tau = tau_ref[g] * (root * s)
+        tau = tau * (root * s)
         sigma = sigma * s
         tau_ref[g] = tau
         sig_ref[g] = sigma
-        return tau, sigma
-
-    def sweep(g, other, tau, closing):
-        wtau = wide(tau)
-        tau1 = wtau[0:1]
+        return s, tau, sigma
+
+    def sweep(g, other, scale, tau, closing):
+        wscale, wtwice = wide(scale), wide(tau + tau)
         ghost_a, ghost_b = shrink(
-            grow[g, 0] + tau1 * slope_row[g, 0], grow[g, 1] + tau1 * slope_row[g, 1], tau1 * cost_row_in[...]
+            wscale * grow[g, 0] + slope_row[g, 0], wscale * grow[g, 1] + slope_row[g, 1], row8(cost_row_in[...])
         )
         side_a, side_b = shrink(
-            gcol[g, 0] + tau * slope_col[g, 0], gcol[g, 1] + tau * slope_col[g, 1], tau * cost_col_in[...]
+            scale * gcol[g, 0] + slope_col[g, 0], scale * gcol[g, 1] + slope_col[g, 1], cost_col_in[...]
         )
         grow[g, 0] = ghost_a
         grow[g, 1] = ghost_b
@@ -397,16 +397,16 @@
 
         def dual(t, a2, above, b2):
             nonlocal acc_d
-            q2 = divergence(t, a2, above, b2, side_b)
-            w = (q2 + q2) - E[g, t]
+            q2 = wtwice * divergence(t, a2, above, b2, side_b)
+            w = q2 - E[g, t]
             W[g, t] = w
             if closing:
-                w = q2 - IM[g, t]
+                w = 0.5 * q2 - IM[g, t]
             acc_d = acc_d + w * w
 
         for t in range(T):
-            a, b = A[g, t], B[g, t]
-            a2, b2 = shrink(a + wtau * GA[g, t], b + wtau * GB[g, t], wtau * CO[t])
+            a, b = wscale * A[g, t], wscale * B[g, t]
+            a2, b2 = shrink(a + GA[g, t], b + GB[g, t], CO[t])
             A[g, t] = a2
             B[g, t] = b2
             if not closing:
@@ -478,7 +478,7 @@
         def _():
             wait_edges(out_sem.at[1], out_sem.at[2], 1)
 
-        sweep(g, 1, step, False)
+        sweep(g, 1, 1.0 / step, step, False)
         depart(1, g, step)
         return c
 
@@ -491,8 +491,8 @@
         other = 1 - slot
 
         def one(g, c):
-            tau, sigma = adapt(slot, g)
-            sweep(g, other, tau, False)
+            s, tau, sigma = adapt(slot, g)
+            sweep(g, other, s, tau, False)
             depart(other, g, sigma)
 
             @pl.when(g < G - 1)
@@ -510,7 +510,8 @@
     slot = (ITERS - 1) % 2
 
     def close(g, c):
-        sweep(g, 1 - slot, adapt(slot, g)[0], True)
+        s, tau, _ = adapt(slot, g)
+        sweep(g, 1 - slot, s, tau, True)
 
         @pl.when(g < G - 1)
         def _():
@@ -519,10 +520,10 @@
         return c
 
     def unload(g, c):
-        wsigma = wide(sig_ref[g])
-        for t in range(T):
-            scatter(flow_in, A[g, t], 0, g, t)
-            scatter(flow_in, B[g, t], 1, g, t)
+        wtau, wsigma = wide(tau_ref[g]), wide(sig_ref[g])
+        for t in range(T):
+            scatter(flow_in, wtau * A[g, t], 0, g, t)
+            scatter(flow_in, wtau * B[g, t], 1, g, t)
             scatter(u_in, U[g, t] + wsigma * W[g, t], g, t)
         return c
 
@@ -598,8 +599,8 @@
             pltpu.VMEM((G, 2, 1, cols), f32), pltpu.VMEM((G, 2) + packed, f32),
             pltpu.VMEM((1, cols), f32), pltpu.VMEM(packed, f32),
             pltpu.VMEM((1, cols), f32), pltpu.VMEM(packed, f32),
-            pltpu.VMEM((G, 2, 1, cols), f32), pltpu.VMEM((G, 2) + packed, f32),
-            pltpu.VMEM((G, 2, 1, cols), f32), pltpu.VMEM((G, 2) + packed, f32),
+            pltpu.VMEM((G, 2, SUBS, cols), f32), pltpu.VMEM((G, 2) + packed, f32),
+            pltpu.VMEM((G, 2, SUBS, cols), f32), pltpu.VMEM((G, 2) + packed, f32),
             pltpu.VMEM(packed, f32), pltpu.VMEM((2 * K + 2 * SUBS + 2, 1, LANES), f32),
             pltpu.SemaphoreType.DMA((G,)), pltpu.SemaphoreType.DMA((2, G)),
             pltpu.SemaphoreType.DMA((G,)), pltpu.SemaphoreType.DMA((2, G)),

time: 71 us -> 71 us (level)
  no operation moved by 1% of the time
where the time goes in v5:
time: 71 us; the launch traced here: 70.9 us
  Pallas kernels  70.2 us (99%)
    pallas_call x1, Pallas kernels, local(): pl.pallas_call(functools.partial(kernel, ny, nx), out_shape=(jax.ShapeDty...  68.5 us
    pallas_call x1, Pallas kernels, local(): pl.pallas_call(finish, out_shape=(jax.ShapeDtypeStruct(flow.shape, f32),...  1.7 us

profile of v5, /device:TPU:0, one launch (start us, length us, event | category | flops | bytes accessed | tf_op | source)
XLA Modules:
  0.0 70.9 jit_solution(1393580910087345104)
XLA Ops:
  0.6 68.5 %shard_map.67 = (f32[2,4,128,512]{3,2,1,0:T(8,128)S(1)}, f32[4,128,512]{2,1,0:T(8,128)S(1)}, f32[8,128]{1,0:T(8,128)S(1)}) custom-call(f32[4,128,512]{2,1,0:T(8,128)} %imb_hbm.1, f32[2,4,128,512]{3,2,1,0:T(8,128)} %flow_hbm.1, f32[4,128,512]{2,1,0:T(8,128)} %u_hbm.1, f32[128,512]{1,0:T(8,128)} %cost_hbm.1), custom_call_target="tpu_custom_call" | custom-call | tf_op jit(solution)/shard_map/pallas_call | solution.py:579
  69.2 1.7 %shard_map.68 = (f32[2,4,128,512]{3,2,1,0:T(8,128)}, f32[4,128,512]{2,1,0:T(8,128)}, f32[1,4]{1,0:T(1,128)}) custom-call(f32[2,4,128,512]{3,2,1,0:T(8,128)S(1)} %get-tuple-element.9.flow_in, f32[4,128,512]{2,1,0:T(8,128)S(1)} %get-tuple-element.10.u_in, f32[8,128]{1,0:T(8,128)S(1)} %get-tuple-element.11.res_in), custom_call_target="tpu_custom_call" | custom-call | tf_op jit(solution)/shard_map/pallas_call | solution.py:614
